TPU v7x, 32 devices: a 4x4x1 block of a 4x4x8 slice. The times are simulated.
32 devices in a mesh: dp: 1 (over z), cpo: 4 (over y), cpi: 8 (over x, core).
Axes of the slice: x: 4, y: 4, z: 1, core: 2. Of those that a mesh axis runs over, the one named last changes fastest.
The devices are a block of a 4x4x8 slice.
Arguments:
- hidden: bfloat16 [8192, 4096], P(('dp', 'cpo', 'cpi'))
- w_query: bfloat16 [4096, 32, 128], replicated
- w_key: bfloat16 [4096, 32, 128], replicated
- w_value: bfloat16 [4096, 32, 128], replicated
- w_out: bfloat16 [32, 128, 4096], replicated
Outputs:
- output: bfloat16 [8192, 4096], P(('dp', 'cpo', 'cpi'))
All inputs are finite; a program needn't handle non-finite values.
Results may differ from a plain program's by a relative error of at most 0.00592155.
Values are sent between devices in bfloat16 or wider.
A program may use at most 768 MiB of HBM per device.

v0:
```python
import jax
import jax.numpy as jnp
from jax import lax
from jax.sharding import PartitionSpec as P

ROPE_BASE = 500000.0
NEG_BIG = -1e30


def rope_tables(positions, head_dim):
    half_dim = head_dim // 2
    inv_freq = ROPE_BASE ** (-(2.0 / head_dim) * jnp.arange(half_dim, dtype=jnp.float32))
    angles = positions.astype(jnp.float32)[..., None] * inv_freq
    return jnp.cos(angles), jnp.sin(angles)


def apply_rope(proj_in, cos_b, sin_b):
    half_dim = proj_in.shape[-1] // 2
    lower_half = proj_in[..., :half_dim]
    upper_half = proj_in[..., half_dim:]
    return jnp.concatenate([lower_half * cos_b - upper_half * sin_b, upper_half * cos_b + lower_half * sin_b], axis=-1)


def softmax_update(state_in, q_blk, q_pos, keys_blk, values_blk, k_pos, score_scale):
    run_max, run_sum, acc_sum = state_in
    scores = jnp.einsum('qkgd,skd->qkgs', q_blk, keys_blk, preferred_element_type=jnp.float32) * score_scale
    causal = k_pos[None, None, None, :] <= q_pos[:, None, None, None]
    scores = jnp.where(causal, scores, -jnp.inf)
    new_max = jnp.maximum(run_max, scores.max(axis=-1))
    probs_blk = jnp.exp(scores - new_max[..., None])
    rescale = jnp.exp(run_max - new_max)
    new_sum = run_sum * rescale + probs_blk.sum(axis=-1)
    new_acc = acc_sum * rescale[..., None] + jnp.einsum('qkgs,skd->qkgd', probs_blk.astype(jnp.bfloat16), values_blk, preferred_element_type=jnp.float32)
    return new_max, new_sum, new_acc


def solution(mesh):
    n_outer = mesh.shape['cpo']
    n_inner = mesh.shape['cpi']
    n_dev = n_outer * n_inner
    shift_perm = [(idx, (idx + 1) % n_outer) for idx in range(n_outer)]

    def device_step(hidden, w_query, w_key, w_value, w_out):
        tok_rows, model_dim = hidden.shape
        chunk_len = tok_rows // 2
        q_heads = w_query.shape[1]
        head_dim = w_query.shape[2]
        kv_heads = w_key.shape[1]
        group_size = q_heads // kv_heads
        kv_loc = kv_heads // n_inner
        heads_loc = q_heads // n_inner
        block_len = n_inner * chunk_len
        score_scale = head_dim ** -0.5
        outer_idx = lax.axis_index('cpo')
        dev_rank = outer_idx * n_inner + lax.axis_index('cpi')
        offsets = jnp.arange(chunk_len, dtype=jnp.int32)
        local_pos = jnp.stack([dev_rank * chunk_len + offsets, (2 * n_dev - 1 - dev_rank) * chunk_len + offsets])
        cos_t, sin_t = rope_tables(local_pos, head_dim)
        cos_b = cos_t[:, :, None, :]
        sin_b = sin_t[:, :, None, :]
        x_halves = hidden.reshape(2, chunk_len, model_dim)
        q_proj = jnp.einsum('veo,ojf->vejf', x_halves, w_query, preferred_element_type=jnp.float32)
        k_proj = jnp.einsum('veo,ojf->vejf', x_halves, w_key, preferred_element_type=jnp.float32)
        v_proj = jnp.einsum('veo,ojf->vejf', x_halves, w_value, preferred_element_type=jnp.float32)
        queries = apply_rope(q_proj, cos_b, sin_b).astype(jnp.bfloat16)
        keys_loc = apply_rope(k_proj, cos_b, sin_b).astype(jnp.bfloat16)
        values_loc = v_proj.astype(jnp.bfloat16)

        def to_heads(tensor_in):
            tensor_in = tensor_in.reshape(2, 1, chunk_len, tensor_in.shape[2], head_dim)
            tensor_in = lax.all_to_all(tensor_in, 'cpi', 3, 1, tiled=True)
            return tensor_in.reshape(2, block_len, tensor_in.shape[3], head_dim)

        queries_h = to_heads(queries).reshape(2, block_len, kv_loc, group_size, head_dim)
        keys_h = to_heads(keys_loc)
        values_h = to_heads(values_loc)
        q_front = queries_h[0]
        q_back = queries_h[1]
        flat_idx = jnp.arange(block_len, dtype=jnp.int32)

        def block_positions(block_idx):
            front_pos = block_idx * block_len + flat_idx
            back_pos = (2 * n_dev - 1 - block_idx * n_inner - flat_idx // chunk_len) * chunk_len + flat_idx % chunk_len
            return front_pos, back_pos

        q_front_pos, q_back_pos = block_positions(outer_idx)

        def empty_state():
            stat_shape = (block_len, kv_loc, group_size)
            return (jnp.full(stat_shape, NEG_BIG, jnp.float32), jnp.zeros(stat_shape, jnp.float32), jnp.zeros(stat_shape + (head_dim,), jnp.float32))

        def attend_block(states, kv_block, src_idx):
            front_state, back_state = states
            keys_blk, values_blk = kv_block
            k_front_pos, k_back_pos = block_positions(src_idx)
            keys_front = keys_blk[0]
            values_front = values_blk[0]
            keys_both = keys_blk.reshape(2 * block_len, kv_loc, head_dim)
            values_both = values_blk.reshape(2 * block_len, kv_loc, head_dim)
            pos_both = jnp.concatenate([k_front_pos, k_back_pos])
            front_state = lax.cond(src_idx <= outer_idx, lambda state_in: softmax_update(state_in, q_front, q_front_pos, keys_front, values_front, k_front_pos, score_scale), lambda state_in: state_in, front_state)
            back_state = lax.cond(src_idx >= outer_idx, lambda state_in: softmax_update(state_in, q_back, q_back_pos, keys_both, values_both, pos_both, score_scale), lambda state_in: softmax_update(state_in, q_back, q_back_pos, keys_front, values_front, k_front_pos, score_scale), back_state)
            return front_state, back_state

        states = attend_block((empty_state(), empty_state()), (keys_h, values_h), outer_idx)

        def outer_step(step_idx, carry_in):
            states_in, kv_block = carry_in
            kv_block = lax.ppermute(kv_block, 'cpo', shift_perm)
            src_idx = (outer_idx - step_idx) % n_outer
            return attend_block(states_in, kv_block, src_idx), kv_block

        final_carry = lax.fori_loop(1, n_outer, outer_step, (states, (keys_h, values_h)))
        front_state, back_state = final_carry[0]
        out_front = (front_state[2] / front_state[1][..., None]).astype(jnp.bfloat16)
        out_back = (back_state[2] / back_state[1][..., None]).astype(jnp.bfloat16)
        out_heads = jnp.stack([out_front, out_back]).reshape(2, n_inner, chunk_len, heads_loc, head_dim)
        out_seq = lax.all_to_all(out_heads, 'cpi', 1, 3, tiled=True).reshape(tok_rows, q_heads, head_dim)
        result = jnp.einsum('thd,hdm->tm', out_seq, w_out, preferred_element_type=jnp.float32)
        return result.astype(jnp.bfloat16)

    row_spec = P(('dp', 'cpo', 'cpi'), None)
    weight_spec = P(None, None, None)
    return jax.shard_map(device_step, mesh=mesh, in_specs=(row_spec, weight_spec, weight_spec, weight_spec, weight_spec), out_specs=row_spec, check_vma=False)
```

profile of v0, /device:TPU:97, one launch (start us, length us, event | category | flops | bytes accessed | tf_op | source)
XLA Modules:
  0.0 805.3 jit_solution(7536123129086082131)
XLA Ops:
  0.0 42.9 %copy.34 = bf16[4096,32,128]{0,2,1:T(8,128)(2,1)} copy(bf16[4096,32,128]{2,1,0:T(8,128)(2,1)} %param.12) | data formatting | bytes 67108864 | tf_op args[1]
  42.9 42.7 %copy.31 = bf16[4096,32,128]{0,2,1:T(8,128)(2,1)} copy(bf16[4096,32,128]{2,1,0:T(8,128)(2,1)} %param.13) | data formatting | bytes 67108864 | tf_op args[2]
  124.9 23.5 %convert_bitcast_fusion = bf16[2,1,128,32,128]{4,2,3,0,1:T(8,128)(2,1)} fusion(bf16[2,128,4096,1]{2,1,3,0:T(8,128)(2,1)S(1)} %bitcast.265, bf16[4096,32,128]{2,1,0:T(8,128)(2,1)} %param.14), kind=kOutput, calls=%fused_computation.114 | convolution fusion | flops 8590983168 | bytes 37748736 | tf_op jit(solution)/shard_map/veo,ojf->vejf/dot_general | solution.py:64
  159.4 23.0 %all-to-all-done.2 = bf16[2,1,128,32,128]{4,2,0,1,3:T(8,128)(2,1)S(1)} async-done(((bf16[2,1,128,32,128]{4,2,0,1,3:T(8,128)(2,1)}), bf16[2,1,128,32,128]{4,2,0,1,3:T(8,128)(2,1)S(1)}, u32[]{:S(2)}, u32[]{:S(2)}) %all-to-all-start.2) | async-done | bytes 2097184 | tf_op jit(solution)/shard_map/all_to_all | solution.py:71
  246.8 16.1 %fusion.74 = (f32[1024,4]{0,1:T(4,128)S(1)}, f32[4,2048,1024]{2,1,0:T(8,128)}) fusion(pred[1024,2048]{0,1:T(8,128)(4,1)} %broadcast_compare_fusion.3, bf16[2048,4,128]{2,0,1:T(8,128)(2,1)} %bitcast.283, bf16[1024,4,128]{2,0,1:T(8,128)(2,1)S(1)} %bitcast.268), kind=kOutput, calls=%fused_computation.92 | convolution fusion | flops 2172645376 | bytes 38813696 | tf_op jit(solution)/shard_map/cond/branch_1_fun/qkgd,skd->qkgs/dot_general | solution.py:26
  281.5 17.4 %bitcast_add_fusion.6 = f32[1024,4,1,128]{0,3,1,2:T(8,128)} fusion(bf16[2048,4,128]{0,2,1:T(8,128)(2,1)} %reshape_reshape.8, f32[4,2048,1024]{2,1,0:T(8,128)} %get-tuple-element.868, f32[1024,4]{0,1:T(4,128)S(1)} %get-tuple-element.859, pred[1024,2048]{0,1:T(8,128)(4,1)} %broadcast_compare_fusion.3, f32[1024,4]{0,1:T(4,128)S(1)} %get-tuple-element.857), kind=kOutput, calls=%fused_computation.110 | convolution fusion | flops 2181562368 | bytes 39878656 | tf_op jit(solution)/shard_map/cond/branch_1_fun/qkgs,skd->qkgd/dot_general | solution.py:33
  301.7 451.9 %while.34 = (s32[]{:T(128)}, f32[1024,4,1]{0,1,2:T(4,128)}, f32[1024,4,1]{0,1,2:T(4,128)}, f32[1024,4,1,128]{3,0,1,2:T(8,128)}, f32[1024,4,1]{0,1,2:T(4,128)S(1)...) while((s32[]{:T(128)}, f32[1024,4,1]{0,1,2:T(4,128)}, ...), condition=%wide.region_15.16_spmd.clone.clone, body=%wide.region_4.15_spmd.clone.clone.sunk | while | flops 6586165248 | bytes 235664336 | solution.py:113
  306.0 45.1 %collective-permute-done = bf16[2,1024,4,128]{3,1,0,2:T(8,128)(2,1)} collective-permute-done((bf16[2,1024,4,128]{3,1,0,2:T(8,128)(2,1)}, bf16[2,1024,4,128]{3,1,0,2:T(8,128)(2,1)}, u32[]{:S(2)}, u32[]{:S(2)}) %collective-permute-start) | collective-permute-done | bytes 2097184 | tf_op jit(solution)/shard_map/while/body/eval_jaxpr/ppermute | solution.py:109
  352.4 43.6 %collective-permute-done.1 = bf16[2,1024,4,128]{3,1,0,2:T(8,128)(2,1)} collective-permute-done((bf16[2,1024,4,128]{3,1,0,2:T(8,128)(2,1)}, bf16[2,1024,4,128]{3,1,0,2:T(8,128)(2,1)}, u32[]{:S(2)}, u32[]{:S(2)}) %collective-permute-start.1) | collective-permute-done | bytes 2097184 | tf_op jit(solution)/shard_map/while/body/eval_jaxpr/ppermute | solution.py:109
  397.4 49.9 %conditional.9 = (f32[1024,4,1]{0,1,2:T(4,128)}, f32[1024,4,1]{0,1,2:T(4,128)S(1)}, f32[1024,4,1,128]{3,0,1,2:T(8,128)}) conditional(s32[]{:T(128)} %convert_element_type.126, (s32[1024]{0:T(1024)S(1)}, s32[1024]{0:T(1024)S(1)}, bf16[1024,4,1,128]{3,0,1,2:T(8,128)(2,1)S(1)}, bf16[1024,4,128]{2,0,1:T(8,128)(2,1)S(1)}, f32[1024,4,1]{0,1,2:T(4,128)S(1)}, ...), branch_computations={%region_9.11_spmd, %region_12.14_spmd} | conditional | flops 4390400000 | bytes 135508064 | solution.py:102
  399.4 15.2 %fusion.40 = (f32[1024,4]{0,1:T(4,128)S(1)}, f32[4,2048,1024]{2,1,0:T(8,128)}) fusion(pred[1024,2048]{0,1:T(8,128)(4,1)S(1)} %broadcast_compare_fusion.2, bf16[2048,4,128]{2,0,1:T(8,128)(2,1)} %bitcast.22, bf16[1024,4,1,128]{3,0,1,2:T(8,128)(2,1)S(1)} %get-tuple-element.647), kind=kOutput, calls=%fused_computation.46 | convolution fusion | flops 2172645376 | bytes 38813696 | tf_op jit(solution)/shard_map/while/body/eval_jaxpr/cond/branch_1_fun/qkgd,skd->qkgs/dot_general | solution.py:26
  430.5 15.4 %bitcast_add_fusion.4 = f32[1024,4,1,128]{3,0,1,2:T(8,128)S(1)} fusion(f32[1024,4,1,128]{3,0,1,2:T(8,128)S(1)} %copy-done.8, bf16[2048,4,128]{2,0,1:T(8,128)(2,1)} %bitcast.31, f32[4,2048,1024]{2,1,0:T(8,128)} %get-tuple-element.846, f32[1024,4]{0,1:T(4,128)} %bitcast.27, pred[1024,2048]{0,1:T(8,128)(4,1)S(1)} %broadcast_compare_fusion.2, ...), kind=kOutput, calls=%fused_computation.51 | convolution fusion | flops 2182086656 | bytes 41975808 | tf_op jit(solution)/shard_map/while/body/eval_jaxpr/cond/branch_1_fun/qkgs,skd->qkgd/dot_general | solution.py:33
  455.1 46.0 %collective-permute-done = bf16[2,1024,4,128]{3,1,0,2:T(8,128)(2,1)} collective-permute-done((bf16[2,1024,4,128]{3,1,0,2:T(8,128)(2,1)}, bf16[2,1024,4,128]{3,1,0,2:T(8,128)(2,1)}, u32[]{:S(2)}, u32[]{:S(2)}) %collective-permute-start) | collective-permute-done | bytes 2097184 | tf_op jit(solution)/shard_map/while/body/eval_jaxpr/ppermute | solution.py:109
  502.4 43.6 %collective-permute-done.1 = bf16[2,1024,4,128]{3,1,0,2:T(8,128)(2,1)} collective-permute-done((bf16[2,1024,4,128]{3,1,0,2:T(8,128)(2,1)}, bf16[2,1024,4,128]{3,1,0,2:T(8,128)(2,1)}, u32[]{:S(2)}, u32[]{:S(2)}) %collective-permute-start.1) | collective-permute-done | bytes 2097184 | tf_op jit(solution)/shard_map/while/body/eval_jaxpr/ppermute | solution.py:109
  547.4 49.9 %conditional.9 = (f32[1024,4,1]{0,1,2:T(4,128)}, f32[1024,4,1]{0,1,2:T(4,128)S(1)}, f32[1024,4,1,128]{3,0,1,2:T(8,128)}) conditional(s32[]{:T(128)} %convert_element_type.126, (s32[1024]{0:T(1024)S(1)}, s32[1024]{0:T(1024)S(1)}, bf16[1024,4,1,128]{3,0,1,2:T(8,128)(2,1)S(1)}, bf16[1024,4,128]{2,0,1:T(8,128)(2,1)S(1)}, f32[1024,4,1]{0,1,2:T(4,128)S(1)}, ...), branch_computations={%region_9.11_spmd, %region_12.14_spmd} | conditional | flops 4390400000 | bytes 135508064 | solution.py:102
  549.4 15.2 %fusion.40 = (f32[1024,4]{0,1:T(4,128)S(1)}, f32[4,2048,1024]{2,1,0:T(8,128)}) fusion(pred[1024,2048]{0,1:T(8,128)(4,1)S(1)} %broadcast_compare_fusion.2, bf16[2048,4,128]{2,0,1:T(8,128)(2,1)} %bitcast.22, bf16[1024,4,1,128]{3,0,1,2:T(8,128)(2,1)S(1)} %get-tuple-element.647), kind=kOutput, calls=%fused_computation.46 | convolution fusion | flops 2172645376 | bytes 38813696 | tf_op jit(solution)/shard_map/while/body/eval_jaxpr/cond/branch_1_fun/qkgd,skd->qkgs/dot_general | solution.py:26
  580.5 15.4 %bitcast_add_fusion.4 = f32[1024,4,1,128]{3,0,1,2:T(8,128)S(1)} fusion(f32[1024,4,1,128]{3,0,1,2:T(8,128)S(1)} %copy-done.8, bf16[2048,4,128]{2,0,1:T(8,128)(2,1)} %bitcast.31, f32[4,2048,1024]{2,1,0:T(8,128)} %get-tuple-element.846, f32[1024,4]{0,1:T(4,128)} %bitcast.27, pred[1024,2048]{0,1:T(8,128)(4,1)S(1)} %broadcast_compare_fusion.2, ...), kind=kOutput, calls=%fused_computation.51 | convolution fusion | flops 2182086656 | bytes 41975808 | tf_op jit(solution)/shard_map/while/body/eval_jaxpr/cond/branch_1_fun/qkgs,skd->qkgd/dot_general | solution.py:33
  605.2 45.2 %collective-permute-done = bf16[2,1024,4,128]{3,1,0,2:T(8,128)(2,1)} collective-permute-done((bf16[2,1024,4,128]{3,1,0,2:T(8,128)(2,1)}, bf16[2,1024,4,128]{3,1,0,2:T(8,128)(2,1)}, u32[]{:S(2)}, u32[]{:S(2)}) %collective-permute-start) | collective-permute-done | bytes 2097184 | tf_op jit(solution)/shard_map/while/body/eval_jaxpr/ppermute | solution.py:109
  651.7 43.6 %collective-permute-done.1 = bf16[2,1024,4,128]{3,1,0,2:T(8,128)(2,1)} collective-permute-done((bf16[2,1024,4,128]{3,1,0,2:T(8,128)(2,1)}, bf16[2,1024,4,128]{3,1,0,2:T(8,128)(2,1)}, u32[]{:S(2)}, u32[]{:S(2)}) %collective-permute-start.1) | collective-permute-done | bytes 2097184 | tf_op jit(solution)/shard_map/while/body/eval_jaxpr/ppermute | solution.py:109
  696.6 49.9 %conditional.9 = (f32[1024,4,1]{0,1,2:T(4,128)}, f32[1024,4,1]{0,1,2:T(4,128)S(1)}, f32[1024,4,1,128]{3,0,1,2:T(8,128)}) conditional(s32[]{:T(128)} %convert_element_type.126, (s32[1024]{0:T(1024)S(1)}, s32[1024]{0:T(1024)S(1)}, bf16[1024,4,1,128]{3,0,1,2:T(8,128)(2,1)S(1)}, bf16[1024,4,128]{2,0,1:T(8,128)(2,1)S(1)}, f32[1024,4,1]{0,1,2:T(4,128)S(1)}, ...), branch_computations={%region_9.11_spmd, %region_12.14_spmd} | conditional | flops 4390400000 | bytes 135508064 | solution.py:102
  698.7 15.3 %fusion.40 = (f32[1024,4]{0,1:T(4,128)S(1)}, f32[4,2048,1024]{2,1,0:T(8,128)}) fusion(pred[1024,2048]{0,1:T(8,128)(4,1)S(1)} %broadcast_compare_fusion.2, bf16[2048,4,128]{2,0,1:T(8,128)(2,1)} %bitcast.22, bf16[1024,4,1,128]{3,0,1,2:T(8,128)(2,1)S(1)} %get-tuple-element.647), kind=kOutput, calls=%fused_computation.46 | convolution fusion | flops 2172645376 | bytes 38813696 | tf_op jit(solution)/shard_map/while/body/eval_jaxpr/cond/branch_1_fun/qkgd,skd->qkgs/dot_general | solution.py:26
  729.8 15.4 %bitcast_add_fusion.4 = f32[1024,4,1,128]{3,0,1,2:T(8,128)S(1)} fusion(f32[1024,4,1,128]{3,0,1,2:T(8,128)S(1)} %copy-done.8, bf16[2048,4,128]{2,0,1:T(8,128)(2,1)} %bitcast.31, f32[4,2048,1024]{2,1,0:T(8,128)} %get-tuple-element.846, f32[1024,4]{0,1:T(4,128)} %bitcast.27, pred[1024,2048]{0,1:T(8,128)(4,1)S(1)} %broadcast_compare_fusion.2, ...), kind=kOutput, calls=%fused_computation.51 | convolution fusion | flops 2182086656 | bytes 41975808 | tf_op jit(solution)/shard_map/while/body/eval_jaxpr/cond/branch_1_fun/qkgs,skd->qkgd/dot_general | solution.py:33
  757.7 31.8 %all_to_all.60 = bf16[2,8,128,4,128]{4,2,0,3,1:T(8,128)(2,1)S(1)} all-to-all(bf16[2,8,128,4,128]{4,2,0,3,1:T(8,128)(2,1)S(1)} %copy.56), channel_id=1, replica_groups=mesh['dp'=1,'cpo'=4,'cpi'=8] {'cpi'}, dimensions={1} | all-to-all | bytes 4194304 | tf_op jit(solution)/shard_map/all_to_all | solution.py:118
  789.4 15.6 %fusion.86 = bf16[256,4096]{1,0:T(8,128)(2,1)} fusion(bf16[256,32,128]{2,0,1:T(8,128)(2,1)S(1)} %bitcast.286, bf16[32,128,4096]{2,1,0:T(8,128)(2,1)} %param.15), kind=kOutput, calls=%fused_computation.105 | convolution fusion | flops 8590983168 | bytes 37748736 | tf_op jit(solution)/shard_map/thd,hdm->tm/dot_general | solution.py:119
  (132 shorter events, 231.9 us)
Async XLA Ops:
  0.0 85.6 %copy-start = (bf16[256,4096]{1,0:T(8,128)(2,1)S(1)}, bf16[256,4096]{1,0:T(8,128)(2,1)}, u32[]{:S(2)}) copy-start(bf16[256,4096]{1,0:T(8,128)(2,1)} %param.11) | copy-start | bytes 6291460
  118.3 33.2 %all-to-all-start = ((bf16[2,1,128,32,128]{2,4,0,1,3:T(8,128)(2,1)}), bf16[2,1,128,32,128]{2,4,0,1,3:T(8,128)(2,1)}, u32[]{:S(2)}, u32[]{:S(2)}) async-start(bf16[2,1,128,32,128]{2,4,0,1,3:T(8,128)(2,1)} %copy.32), calls=%async_computation | async-start | bytes 4194304 | tf_op jit(solution)/shard_map/all_to_all | solution.py:71
  151.5 30.9 %all-to-all-start.2 = ((bf16[2,1,128,32,128]{4,2,0,1,3:T(8,128)(2,1)}), bf16[2,1,128,32,128]{4,2,0,1,3:T(8,128)(2,1)S(1)}, u32[]{:S(2)}, u32[]{:S(2)}) async-start(bf16[2,1,128,32,128]{4,2,0,1,3:T(8,128)(2,1)} %copy.38), calls=%async_computation.2 | async-start | bytes 4194304 | tf_op jit(solution)/shard_map/all_to_all | solution.py:71
  182.4 8.8 %copy-start.7 = (bf16[2,1,128,32,128]{4,2,0,1,3:T(8,128)(2,1)}, bf16[2,1,128,32,128]{4,2,0,1,3:T(8,128)(2,1)S(1)}, u32[]{:S(2)}) copy-start(bf16[2,1,128,32,128]{4,2,0,1,3:T(8,128)(2,1)S(1)} %all-to-all-done.2) | copy-start | bytes 6291460
  182.4 31.9 %all-to-all-start.1 = ((bf16[2,1,128,32,128]{2,4,0,1,3:T(8,128)(2,1)}), bf16[2,1,128,32,128]{2,4,0,1,3:T(8,128)(2,1)}, u32[]{:S(2)}, u32[]{:S(2)}) async-start(bf16[2,1,128,32,128]{2,4,0,1,3:T(8,128)(2,1)} %copy.35), calls=%async_computation.1 | async-start | bytes 4194304 | tf_op jit(solution)/shard_map/all_to_all | solution.py:71
  218.2 1.9 copy-start.10
  223.1 5.7 copy-start.4
  246.8 16.1 %copy-start.5 = (pred[1024,2048]{0,1:T(8,128)(4,1)S(1)}, pred[1024,2048]{0,1:T(8,128)(4,1)}, u32[]{:S(2)}) copy-start(pred[1024,2048]{0,1:T(8,128)(4,1)} %broadcast_compare_fusion.3) | copy-start | bytes 6291460
  301.9 4.1 copy-start.2
  301.9 49.2 %collective-permute-start = (bf16[2,1024,4,128]{3,1,0,2:T(8,128)(2,1)}, bf16[2,1024,4,128]{3,1,0,2:T(8,128)(2,1)}, u32[]{:S(2)}, u32[]{:S(2)}) collective-permute-start(bf16[2,1024,4,128]{3,1,0,2:T(8,128)(2,1)} %get-tuple-element.1014), channel_id=1, source_target_pairs={{0,8},{8,16},{16,24},{24,0},{1,9},{9,17},{17,25},{25,1},{2,10},{10... | collective-permute-start | bytes 6291464 | tf_op jit(solution)/shard_map/while/body/eval_jaxpr/ppermute | solution.py:109
  303.5 92.5 %collective-permute-start.1 = (bf16[2,1024,4,128]{3,1,0,2:T(8,128)(2,1)}, bf16[2,1024,4,128]{3,1,0,2:T(8,128)(2,1)}, u32[]{:S(2)}, u32[]{:S(2)}) collective-permute-start(bf16[2,1024,4,128]{3,1,0,2:T(8,128)(2,1)} %get-tuple-element.1015), channel_id=1, source_target_pairs={{0,8},{8,16},{16,24},{24,0},{1,9},{9,17},{17,25},{25,1},{2,10},{10... | collective-permute-start | bytes 6291464 | tf_op jit(solution)/shard_map/while/body/eval_jaxpr/ppermute | solution.py:109
  415.3 15.2 %copy-start.8 = (f32[1024,4,1,128]{3,0,1,2:T(8,128)S(1)}, f32[1024,4,1,128]{3,0,1,2:T(8,128)}, u32[]{:S(2)}) copy-start(f32[1024,4,1,128]{3,0,1,2:T(8,128)} %get-tuple-element.649) | copy-start | bytes 6291460 | tf_op jit(solution)/shard_map/while/body/eval_jaxpr/cond
  445.9 1.3 copy-start.9
  448.0 6.2 copy-start.3
  454.2 47.0 %collective-permute-start = (bf16[2,1024,4,128]{3,1,0,2:T(8,128)(2,1)}, bf16[2,1024,4,128]{3,1,0,2:T(8,128)(2,1)}, u32[]{:S(2)}, u32[]{:S(2)}) collective-permute-start(bf16[2,1024,4,128]{3,1,0,2:T(8,128)(2,1)} %get-tuple-element.1014), channel_id=1, source_target_pairs={{0,8},{8,16},{16,24},{24,0},{1,9},{9,17},{17,25},{25,1},{2,10},{10... | collective-permute-start | bytes 6291464 | tf_op jit(solution)/shard_map/while/body/eval_jaxpr/ppermute | solution.py:109
  454.2 91.9 %collective-permute-start.1 = (bf16[2,1024,4,128]{3,1,0,2:T(8,128)(2,1)}, bf16[2,1024,4,128]{3,1,0,2:T(8,128)(2,1)}, u32[]{:S(2)}, u32[]{:S(2)}) collective-permute-start(bf16[2,1024,4,128]{3,1,0,2:T(8,128)(2,1)} %get-tuple-element.1015), channel_id=1, source_target_pairs={{0,8},{8,16},{16,24},{24,0},{1,9},{9,17},{17,25},{25,1},{2,10},{10... | collective-permute-start | bytes 6291464 | tf_op jit(solution)/shard_map/while/body/eval_jaxpr/ppermute | solution.py:109
  565.3 15.2 %copy-start.8 = (f32[1024,4,1,128]{3,0,1,2:T(8,128)S(1)}, f32[1024,4,1,128]{3,0,1,2:T(8,128)}, u32[]{:S(2)}) copy-start(f32[1024,4,1,128]{3,0,1,2:T(8,128)} %get-tuple-element.649) | copy-start | bytes 6291460 | tf_op jit(solution)/shard_map/while/body/eval_jaxpr/cond
  598.0 6.2 copy-start.3
  604.2 46.2 %collective-permute-start = (bf16[2,1024,4,128]{3,1,0,2:T(8,128)(2,1)}, bf16[2,1024,4,128]{3,1,0,2:T(8,128)(2,1)}, u32[]{:S(2)}, u32[]{:S(2)}) collective-permute-start(bf16[2,1024,4,128]{3,1,0,2:T(8,128)(2,1)} %get-tuple-element.1014), channel_id=1, source_target_pairs={{0,8},{8,16},{16,24},{24,0},{1,9},{9,17},{17,25},{25,1},{2,10},{10... | collective-permute-start | bytes 6291464 | tf_op jit(solution)/shard_map/while/body/eval_jaxpr/ppermute | solution.py:109
  604.2 91.1 %collective-permute-start.1 = (bf16[2,1024,4,128]{3,1,0,2:T(8,128)(2,1)}, bf16[2,1024,4,128]{3,1,0,2:T(8,128)(2,1)}, u32[]{:S(2)}, u32[]{:S(2)}) collective-permute-start(bf16[2,1024,4,128]{3,1,0,2:T(8,128)(2,1)} %get-tuple-element.1015), channel_id=1, source_target_pairs={{0,8},{8,16},{16,24},{24,0},{1,9},{9,17},{17,25},{25,1},{2,10},{10... | collective-permute-start | bytes 6291464 | tf_op jit(solution)/shard_map/while/body/eval_jaxpr/ppermute | solution.py:109
  714.6 15.2 %copy-start.8 = (f32[1024,4,1,128]{3,0,1,2:T(8,128)S(1)}, f32[1024,4,1,128]{3,0,1,2:T(8,128)}, u32[]{:S(2)}) copy-start(f32[1024,4,1,128]{3,0,1,2:T(8,128)} %get-tuple-element.649) | copy-start | bytes 6291460 | tf_op jit(solution)/shard_map/while/body/eval_jaxpr/cond
  747.2 6.2 copy-start.3
  753.7 2.2 copy-start.6
  789.4 15.6 %copy-start.1 = (bf16[256,4096]{1,0:T(8,128)(2,1)S(1)}, bf16[256,4096]{1,0:T(8,128)(2,1)}, u32[]{:S(2)}) copy-start(bf16[256,4096]{1,0:T(8,128)(2,1)} %param.11) | copy-start | bytes 6291460
  (4 other events, 4.5 us)
where the time goes:
time: 815 us; the launch traced here: 805 us
  waiting for transfers between devices  299 us (37%)
  matrix products  208 us (26%)
  local copies, waits for them, and re-layouts  158 us (19%)
  other arithmetic  85.8 us (11%)
  blocking collectives  31.8 us (4%)
  starting transfers between devices  20.9 us (3%)
    ppermute x6, waiting for transfers between devices, outer_step(): kv_block = lax.ppermute(kv_block, 'cpo', shift_perm)  267 us
    unnamed x18, local copies, waits for them, and re-layouts  93 us
    dot_general x5, matrix products, softmax_update(): jnp.einsum('qkgs,skd->qkgd', probs_blk.astype(jnp.bfloat16), values_blk,...  75.7 us
    dot_general x5, matrix products, softmax_update(): jnp.einsum('qkgd,skd->qkgs', q_blk, keys_blk, preferred_element_type=jnp....  64.9 us
    reduce_sum x5, other arithmetic, softmax_update(): new_sum = run_sum * rescale + probs_blk.sum(axis=-1)  61.3 us
    all_to_all x3, waiting for transfers between devices, to_heads(): tensor_in = lax.all_to_all(tensor_in, 'cpi', 3, 1, tiled=True)  31.8 us
    all_to_all x1, blocking collectives, device_step(): lax.all_to_all(out_heads, 'cpi', 1, 3, tiled=True)  31.8 us
    dot_general x1, matrix products, device_step(): jnp.einsum('veo,ojf->vejf', x_halves, w_value, preferred_element_type=jnp...  23.5 us
  transfers between devices with their start and end apart: 9, of which 8 were waited for; matrix products, arithmetic and copies ran while one was open for 7% of the time, Pallas kernels for 0%

commit v1 on v0

v1 whole, which is shorter than its diff:
```python
import functools
import math

import jax
import jax.numpy as jnp
from jax import lax
from jax.experimental import pallas as pl
from jax.experimental.pallas import tpu as pltpu
from jax.sharding import PartitionSpec as P

ROPE_BASE = 500000.0
NEG_BIG = -1e30
MESH = pl.DeviceIdType.MESH
PIECES = 8
F32 = jnp.float32
BF16 = jnp.bfloat16


def remote(src, dst, send_sem, recv_sem, y, i):
    return pltpu.make_async_remote_copy(src_ref=src, dst_ref=dst, send_sem=send_sem, recv_sem=recv_sem, device_id={'cpo': y, 'cpi': i}, device_id_type=MESH)


def wait_bytes(ref, sem):
    pltpu.make_async_copy(ref, ref, sem).wait()


def piece_half(p):
    return jnp.where(p < 2, p, jnp.where(p < 4, 0, jnp.where(p < 6, 1, p - 6)))


def piece_dy(p, n_outer):
    return jnp.where(p < 2, 0, jnp.where(p < 6, jnp.where(lax.rem(p, 2) == 0, n_outer - 1, 1), 2))


def qkv_kernel(n_outer, n_inner, hid_in, wq, wk, wv, cos_ref, sin_ref, qkv_out,
               hid_buf, raw, wide, wbuf, stage, relay,
               h_send, h_recv, h_load, w_sem, s_send, l_sem, r_send, r_recv, q_recv):
    y = lax.axis_index('cpo')
    i = lax.axis_index('cpi')
    n_x = n_inner // 2
    x = i // 2
    c = lax.rem(i, 2)
    chunk = hid_buf.shape[1]
    n_chunks = qkv_out.shape[0]
    depth = raw.shape[1]
    n_k = wbuf.shape[1] // depth
    y_up = lax.rem(y + 1, n_outer)
    y_dn = lax.rem(y + n_outer - 1, n_outer)
    x_up = lax.rem(x + 1, n_x)
    x_dn = lax.rem(x + n_x - 1, n_x)
    weights = (wq, wk, wv)
    n_raw = raw.shape[0]

    def w_copy(t, kc, slot):
        src = weights[t].at[pl.ds(kc * depth, depth), pl.ds(pl.multiple_of(y * n_inner, n_inner), n_inner)]
        return pltpu.make_async_copy(src, raw.at[slot], w_sem.at[slot])

    for slot in range(n_raw):
        w_copy(0, slot, slot).start()
    own = [pltpu.make_async_copy(hid_in.at[pl.ds(f * chunk, chunk)], hid_buf.at[f], h_load.at[f]) for f in range(2)]
    for cp in own:
        cp.start()

    barrier = pltpu.get_barrier_semaphore()
    pl.semaphore_signal(barrier, inc=1, device_id={'cpo': y_up, 'cpi': i}, device_id_type=MESH)
    pl.semaphore_signal(barrier, inc=1, device_id={'cpo': y_dn, 'cpi': i}, device_id_type=MESH)
    for d in range(1, n_inner):
        pl.semaphore_signal(barrier, inc=1, device_id={'cpo': y, 'cpi': lax.rem(i + d, n_inner)}, device_id_type=MESH)
    pl.semaphore_wait(barrier, n_inner + 1)

    hid_sends = []
    for f in range(2):
        src = hid_in.at[pl.ds(f * chunk, chunk)]
        hid_sends.append(remote(src, hid_buf.at[2 + 2 * f], h_send.at[2 * f], h_recv.at[2 + 2 * f], y_up, i))
        hid_sends.append(remote(src, hid_buf.at[3 + 2 * f], h_send.at[2 * f + 1], h_recv.at[3 + 2 * f], y_dn, i))
    for cp in hid_sends:
        cp.start()
    fwd_up = remote(hid_buf.at[2], hid_buf.at[6], h_send.at[4], h_recv.at[6], y_up, i)
    fwd_dn = remote(hid_buf.at[5], hid_buf.at[7], h_send.at[5], h_recv.at[7], y_dn, i)

    for t in range(3):
        def relayout(kc, _, t=t):
            slot = lax.rem(t * n_k + kc, n_raw)
            w_copy(t, kc, slot).wait()
            wide[...] = raw[slot].astype(F32)
            for j in range(n_inner):
                col = (j % 2) * 384 + t * 128
                wbuf[j // 2, pl.ds(pl.multiple_of(kc * depth, depth), depth), col:col + 128] = wide[:, j, :].astype(BF16)
            nxt = kc + n_raw

            @pl.when(nxt < n_k)
            def _():
                w_copy(t, nxt, slot).start()

            if t < 2:
                @pl.when(nxt >= n_k)
                def _():
                    w_copy(t + 1, nxt - n_k, slot).start()
            return 0

        lax.fori_loop(0, n_k, relayout, 0)
    for cp in own:
        cp.wait()

    def chunk_index(p, src_i):
        rank = lax.rem(y + piece_dy(p, n_outer), n_outer) * n_inner + src_i
        return jnp.where(piece_half(p) == 0, rank, n_chunks - 1 - rank)

    def relay_copy(p, c2):
        front = piece_half(p) == 0
        src_x = jnp.where(front, x_dn, x_up)
        dst_x = jnp.where(front, x_up, x_dn)
        return remote(relay.at[p, c2], qkv_out.at[chunk_index(p, src_x * 2 + c)], r_send, q_recv, y, dst_x * 2 + c2)

    def forward_relay(p):
        for c2 in range(2):
            wait_bytes_remote = pltpu.make_async_copy(relay.at[p, c2], relay.at[p, c2], r_recv.at[p, c2])
            wait_bytes_remote.wait()
            relay_copy(p, c2).start()

    def piece(p, _):
        @pl.when(jnp.logical_and(p >= 2, p != 5))
        def _():
            wait_bytes(hid_buf.at[p], h_recv.at[p])

        @pl.when(p == 2)
        def _():
            fwd_up.start()

        @pl.when(p == 4)
        def _():
            wait_bytes(hid_buf.at[5], h_recv.at[5])
            fwd_dn.start()

        cos_p = cos_ref[p]
        sin_p = sin_ref[p]

        def rope(a):
            return a * cos_p + pltpu.roll(a, 64, 1) * sin_p

        out_t = chunk_index(p, i)

        def per_chip(kk, _):
            xc = lax.rem(x + jnp.where(kk == 0, 2, jnp.where(kk == 1, 1, jnp.where(kk == 2, n_x - 1, 0))), n_x)
            acc = jnp.dot(hid_buf[p], wbuf[xc], preferred_element_type=F32)
            for c2 in range(2):
                col = c2 * 384
                stage[p, xc * 2 + c2, 0] = rope(acc[:, col:col + 128]).astype(BF16)
                stage[p, xc * 2 + c2, 1] = rope(acc[:, col + 128:col + 256]).astype(BF16)
                stage[p, xc * 2 + c2, 2] = acc[:, col + 256:col + 384].T.astype(BF16)

            @pl.when(kk == 0)
            def _():
                via = jnp.where(piece_half(p) == 0, x_up, x_dn)
                for c2 in range(2):
                    remote(stage.at[p, xc * 2 + c2], relay.at[p, c2], s_send, r_recv.at[p, c2], y, via * 2 + c).start()

            @pl.when(jnp.logical_and(kk >= 1, kk <= 2))
            def _():
                for c2 in range(2):
                    remote(stage.at[p, xc * 2 + c2], qkv_out.at[out_t], s_send, q_recv, y, xc * 2 + c2).start()

            @pl.when(kk == 3)
            def _():
                remote(stage.at[p, xc * 2 + 1 - c], qkv_out.at[out_t], s_send, q_recv, y, xc * 2 + 1 - c).start()
                pltpu.make_async_copy(stage.at[p, i], qkv_out.at[out_t], l_sem).start()
            return 0

        lax.fori_loop(0, n_x, per_chip, 0)

        @pl.when(p >= 1)
        def _():
            forward_relay(p - 1)
        return 0

    lax.fori_loop(0, PIECES, piece, 0)
    forward_relay(PIECES - 1)

    for cp in hid_sends:
        cp.wait_send()
    fwd_up.wait_send()
    fwd_dn.wait_send()
    wait_bytes(stage.at[:, pl.ds(0, n_inner - 1)], s_send)
    wait_bytes(relay, r_send)
    wait_bytes(qkv_out.at[pl.ds(0, PIECES)], l_sem)
    wait_bytes(qkv_out.at[pl.ds(0, n_chunks - PIECES)], q_recv)


def attn_kernel(n_outer, n_inner, score_scale, qkv_hbm, wout_hbm, out_ref,
                qkv, wbuf, s0, s1, m_ref, l_ref, acc_ref, o_stage, o_recv, ld_sem, w_sem, o_send, o_sem):
    y = lax.axis_index('cpo')
    i = lax.axis_index('cpi')
    me = y * n_inner + i
    n_dev = n_outer * n_inner
    head_dim = qkv.shape[2]
    chunk = qkv.shape[3]
    tk, tq = s0.shape
    kc = tk // chunk
    qc = tq // chunk
    n_q = qkv.shape[0] // qc
    strip = 256
    n_strips = tq // strip
    n_w = wbuf.shape[0]
    wide = wbuf.shape[2]
    c_exp = score_scale * math.log2(math.e)

    load = pltpu.make_async_copy(qkv_hbm, qkv, ld_sem)
    load.start()

    barrier = pltpu.get_barrier_semaphore()

    def sig(d, _):
        peer = lax.rem(me + d, n_dev)
        pl.semaphore_signal(barrier, inc=1, device_id={'cpo': peer // n_inner, 'cpi': lax.rem(peer, n_inner)}, device_id_type=MESH)
        return 0

    lax.fori_loop(1, n_dev, sig, 0)
    w_copies = [pltpu.make_async_copy(wout_hbm.at[:, pl.ds(n * wide, wide)], wbuf.at[n], w_sem) for n in range(n_w)]
    for cp in w_copies:
        cp.start()
    load.wait()
    pl.semaphore_wait(barrier, n_dev - 1)

    def k_tile(j):
        return qkv[pl.ds(j * kc, kc), 1].reshape(tk, head_dim)

    def vt_tile(j, rows):
        return jnp.concatenate([qkv[j * kc + u, 2] for u in range(rows // chunk)], axis=1)

    def q_strip(b, st):
        n = strip // chunk
        return qkv[pl.ds(b * qc + st * n, n), 0].reshape(strip, head_dim)

    def scores(dst, b, j, st):
        dst[:, st * strip:(st + 1) * strip] = lax.dot_general(k_tile(j), q_strip(b, st), (((1,), (1,)), ((), ())), preferred_element_type=F32)

    def update(src, j, st, rows, mask_off):
        sl = slice(st * strip, (st + 1) * strip)
        s = src[0:rows, sl]
        if mask_off is not None:
            r = lax.broadcasted_iota(jnp.int32, (rows, strip), 0)
            q = lax.broadcasted_iota(jnp.int32, (rows, strip), 1)
            s = jnp.where(r <= q + mask_off, s, NEG_BIG)
        m_old = m_ref[:, sl]
        m_new = jnp.maximum(m_old, jnp.max(s, axis=0, keepdims=True))
        alpha = jnp.exp2((m_old - m_new) * c_exp)
        p = jnp.exp2((s - m_new) * c_exp)
        l_ref[:, sl] = l_ref[:, sl] * alpha + jnp.sum(p, axis=0, keepdims=True)
        m_ref[:, sl] = m_new
        acc_ref[:, sl] = acc_ref[:, sl] * alpha + jnp.dot(vt_tile(j, rows), p.astype(BF16), preferred_element_type=F32)

    def q_block(n, _):
        row = lax.rem(y + 1 + n // 2, n_outer)
        b = jnp.where(lax.rem(n, 2) == 0, row, n_q - 1 - row)
        m_ref[...] = jnp.full(m_ref.shape, NEG_BIG, F32)
        l_ref[...] = jnp.zeros(l_ref.shape, F32)
        acc_ref[...] = jnp.zeros(acc_ref.shape, F32)
        for st in range(n_strips):
            scores(s0, b, 0, st)

        def pair(jj, _):
            for st in range(n_strips):
                scores(s1, b, 2 * jj + 1, st)
                update(s0, 2 * jj, st, tk, None)
            for st in range(n_strips):
                scores(s0, b, 2 * jj + 2, st)
                update(s1, 2 * jj + 1, st, tk, None)
            return 0

        lax.fori_loop(0, b, pair, 0)
        half = n_strips // 2
        for st in range(n_strips):
            if st >= half:
                scores(s1, b, 2 * b + 1, st)
                update(s0, 2 * b, st, tk, None)
            else:
                update(s0, 2 * b, st, (st + 1) * strip, st * strip)
        for st in range(half, n_strips):
            update(s1, 2 * b + 1, st, (st + 1 - half) * strip, (st - half) * strip)

        inv = 1.0 / l_ref[...]
        for u in range(qc):
            sl = slice(u * chunk, (u + 1) * chunk)
            o_stage[b * qc + u] = (acc_ref[:, sl] * inv[:, sl]).T.astype(BF16)
        cols = pl.ds(pl.multiple_of(me * head_dim, head_dim), head_dim)
        for u in range(qc):
            t = b * qc + u
            front = t < n_dev
            owner = jnp.where(front, t, 2 * n_dev - 1 - t)
            rows = pl.ds(pl.multiple_of(jnp.where(front, 0, chunk), chunk), chunk)

            @pl.when(owner == me)
            def _():
                o_recv[rows, cols] = o_stage[t]

            @pl.when(owner != me)
            def _():
                remote(o_stage.at[t], o_recv.at[rows, cols], o_send, o_sem, owner // n_inner, lax.rem(owner, n_inner)).start()
        return 0

    lax.fori_loop(0, n_q, q_block, 0)
    n_mine = 2 * (n_dev - 1)
    wait_bytes(o_stage.at[pl.ds(0, n_mine)], o_send)
    for cp in w_copies:
        pass
    wait_bytes(wbuf, w_sem)
    wait_bytes(o_stage.at[pl.ds(0, n_mine)], o_sem)

    def out_tile(n, _):
        out_ref[:, pl.ds(pl.multiple_of(n * wide, wide), wide)] = jnp.dot(o_recv[...], wbuf[n], preferred_element_type=F32).astype(BF16)
        return 0

    lax.fori_loop(0, n_w, out_tile, 0)


def solution(mesh):
    n_outer = mesh.shape['cpo']
    n_inner = mesh.shape['cpi']
    n_dev = n_outer * n_inner

    def device_step(hidden, w_query, w_key, w_value, w_out):
        rows, model_dim = hidden.shape
        chunk = rows // 2
        n_heads, head_dim = w_query.shape[1:]
        n_chunks = 2 * n_dev
        y = lax.axis_index('cpo')
        i = lax.axis_index('cpi')
        p = jnp.arange(PIECES, dtype=jnp.int32)
        rank = (y + piece_dy(p, n_outer)) % n_outer * n_inner + i
        t = jnp.where(piece_half(p) == 0, rank, n_chunks - 1 - rank)
        pos = t[:, None] * chunk + jnp.arange(chunk, dtype=jnp.int32)
        half_dim = head_dim // 2
        inv_freq = ROPE_BASE ** (-(2.0 / head_dim) * jnp.arange(half_dim, dtype=F32))
        angles = pos.astype(F32)[..., None] * inv_freq
        cos_t, sin_t = jnp.cos(angles), jnp.sin(angles)
        cos_t = jnp.concatenate([cos_t, cos_t], axis=-1)
        sin_t = jnp.concatenate([-sin_t, sin_t], axis=-1)

        any_spec = pl.BlockSpec(memory_space=pl.ANY)
        vmem_spec = pl.BlockSpec(memory_space=pltpu.VMEM)
        dma = pltpu.SemaphoreType.DMA
        qkv = pl.pallas_call(
            functools.partial(qkv_kernel, n_outer, n_inner),
            out_shape=jax.ShapeDtypeStruct((n_chunks, 3, chunk, head_dim), BF16),
            in_specs=[any_spec] * 4 + [vmem_spec] * 2,
            out_specs=any_spec,
            scratch_shapes=[
                pltpu.VMEM((PIECES, chunk, model_dim), BF16),
                pltpu.VMEM((4, 512, n_inner, head_dim), BF16),
                pltpu.VMEM((512, n_inner, head_dim), F32),
                pltpu.VMEM((n_inner // 2, model_dim, 6 * head_dim), BF16),
                pltpu.VMEM((PIECES, n_inner, 3, chunk, head_dim), BF16),
                pltpu.VMEM((PIECES, 2, 3, chunk, head_dim), BF16),
                dma((6,)), dma((PIECES,)), dma((2,)), dma((4,)), dma, dma, dma, dma((PIECES, 2)), dma,
            ],
            compiler_params=pltpu.CompilerParams(collective_id=0, has_side_effects=True, vmem_limit_bytes=60 * 2**20),
            name='qkv_exchange',
        )(hidden, w_query, w_key, w_value, cos_t, sin_t)

        tk, tq = 512, 1024
        n_w = 8
        return pl.pallas_call(
            functools.partial(attn_kernel, n_outer, n_inner, head_dim ** -0.5),
            out_shape=jax.ShapeDtypeStruct((rows, model_dim), BF16),
            in_specs=[any_spec] * 2,
            out_specs=vmem_spec,
            scratch_shapes=[
                pltpu.VMEM((n_chunks, 3, chunk, head_dim), BF16),
                pltpu.VMEM((n_w, n_heads * head_dim, model_dim // n_w), BF16),
                pltpu.VMEM((tk, tq), F32),
                pltpu.VMEM((tk, tq), F32),
                pltpu.VMEM((1, tq), F32),
                pltpu.VMEM((1, tq), F32),
                pltpu.VMEM((head_dim, tq), F32),
                pltpu.VMEM((n_chunks, chunk, head_dim), BF16),
                pltpu.VMEM((rows, n_heads * head_dim), BF16),
                dma, dma, dma, dma,
            ],
            compiler_params=pltpu.CompilerParams(collective_id=1, has_side_effects=True, vmem_limit_bytes=60 * 2**20),
            name='attn_out',
        )(qkv, w_out.reshape(n_heads * head_dim, model_dim))

    row_spec = P(('dp', 'cpo', 'cpi'), None)
    weight_spec = P(None, None, None)
    return jax.shard_map(device_step, mesh=mesh, in_specs=(row_spec, weight_spec, weight_spec, weight_spec, weight_spec), out_specs=row_spec, check_vma=False)
```

time: 815 us -> 223 us (0.27); the launches traced: 805 us -> 223 us
  waiting for transfers between devices: 299 us -> 0 us
  Pallas kernels: 0 us -> 216 us
  matrix products: 208 us -> 0 us
  local copies, waits for them, and re-layouts: 158 us -> 3.13 us
  other arithmetic: 85.8 us -> 3.32 us
  blocking collectives: 31.8 us -> 0 us
  starting transfers between devices: 20.9 us -> 0 us
    ppermute x6 -> x0, waiting for transfers between devices: 267 us -> none  [outer_step(): kv_block = lax.ppermute(kv_block, 'cpo', shift_perm)]
    pallas_call x0 -> x2, Pallas kernels: none -> 216 us  [the longest x1 148 us: device_step(): pl.pallas_call(functools.partial(qkv_kernel, n_outer, n_inner), out_shape...]
    dot_general x14 -> x0, matrix products: 208 us -> none  [the longest x5 75.7 us: softmax_update(): jnp.einsum('qkgs,skd->qkgd', probs_blk.astype(jnp.bfloat16), values_blk,...]
    unnamed x18 -> x1, local copies, waits for them, and re-layouts: 93 us -> 3.13 us
    reduce_sum x5 -> x0, other arithmetic: 61.3 us -> none  [softmax_update(): new_sum = run_sum * rescale + probs_blk.sum(axis=-1)]
    all_to_all x3 -> x0, waiting for transfers between devices: 31.8 us -> none  [to_heads(): tensor_in = lax.all_to_all(tensor_in, 'cpi', 3, 1, tiled=True)]
    all_to_all x1 -> x0, blocking collectives: 31.8 us -> none  [device_step(): lax.all_to_all(out_heads, 'cpi', 1, 3, tiled=True)]
    while x21 -> x0, local copies, waits for them, and re-layouts: 20.9 us -> none
  transfers between devices with their start and end apart: 9 -> 0, of which waited for: 8 -> 0; matrix products, arithmetic and copies ran while one was open for 7% -> 0% of each run, Pallas kernels for 0% -> 0%
where the time goes in v1:
time: 223 us
  Pallas kernels  216 us (97%)
  other arithmetic  3.32 us (1%)
  local copies, waits for them, and re-layouts  3.13 us (1%)
    pallas_call x1, Pallas kernels, device_step(): pl.pallas_call(functools.partial(qkv_kernel, n_outer, n_inner), out_shape...  148 us
    pallas_call x1, Pallas kernels, device_step(): pl.pallas_call(functools.partial(attn_kernel, n_outer, n_inner, head_dim...  68.4 us

profile of v1, /device:TPU:97, one launch (start us, length us, event | category | flops | bytes accessed | tf_op | source)
XLA Modules:
  0.0 222.5 jit_solution(2698414528970799150)
XLA Ops:
  0.0 0.1 add_convert_fusion
  0.1 1.9 fusion
  2.0 1.3 pad_maximum_fusion
  3.3 147.7 %qkv_exchange.1.qkv_hbm = bf16[64,3,128,128]{3,2,1,0:T(8,128)(2,1)} custom-call(bf16[256,4096]{1,0:T(8,128)(2,1)} %hid_in.1, bf16[4096,32,128]{2,1,0:T(8,128)(2,1)} %wq.1, bf16[4096,32,128]{2,1,0:T(8,128)(2,1)} %wk.1, bf16[4096,32,128]{2,1,0:T(8,128)(2,1)} %wv.1, f32[8,128,128]{2,1,0:T(8,128)} %get-tuple-element.8.cos_ref, ...), custom_call_target="tpu_custom_call" | custom-call | tf_op jit(solution)/shard_map/qkv_exchange/pallas_call | solution.py:342
  151.0 68.4 %attn_out.1 = bf16[256,4096]{1,0:T(8,128)(2,1)} custom-call(bf16[64,3,128,128]{3,2,1,0:T(8,128)(2,1)} %qkv_exchange.1.qkv_hbm, bf16[4096,4096]{1,0:T(8,128)(2,1)} %bitcast.1), custom_call_target="tpu_custom_call" | custom-call | tf_op jit(solution)/shard_map/attn_out/pallas_call | solution.py:362
  219.4 3.1 %copy.7 = bf16[256,4096]{1,0:T(8,128)(2,1)} copy(bf16[256,4096]{1,0:T(8,128)(2,1)} %attn_out.1) | data formatting | bytes 4194304
  (2 shorter events, 0.0 us)

commit v2 on v1

--- a/solution.py
+++ b/solution.py
@@ -82,10 +82,10 @@
         def relayout(kc, _, t=t):
             slot = lax.rem(t * n_k + kc, n_raw)
             w_copy(t, kc, slot).wait()
-            wide[...] = raw[slot].astype(F32)
+            wide[...] = raw[slot].astype(F32).reshape(wide.shape)
             for j in range(n_inner):
                 col = (j % 2) * 384 + t * 128
-                wbuf[j // 2, pl.ds(pl.multiple_of(kc * depth, depth), depth), col:col + 128] = wide[:, j, :].astype(BF16)
+                wbuf[j // 2, pl.ds(pl.multiple_of(kc * depth, depth), depth), col:col + 128] = wide[pl.ds(j, depth, n_inner), :].astype(BF16)
             nxt = kc + n_raw
 
             @pl.when(nxt < n_k)
@@ -187,7 +187,7 @@
 
 
 def attn_kernel(n_outer, n_inner, score_scale, qkv_hbm, wout_hbm, out_ref,
-                qkv, wbuf, s0, s1, m_ref, l_ref, acc_ref, o_stage, o_recv, ld_sem, w_sem, o_send, o_sem):
+                qkv, wbuf, s0, s1, x0, x1, m_ref, l_ref, acc_ref, o_stage, o_recv, ld_sem, w_sem, o_send, o_sem):
     y = lax.axis_index('cpo')
     i = lax.axis_index('cpi')
     me = y * n_inner + i
@@ -231,20 +231,22 @@
         n = strip // chunk
         return qkv[pl.ds(b * qc + st * n, n), 0].reshape(strip, head_dim)
 
-    def scores(dst, b, j, st):
-        dst[:, st * strip:(st + 1) * strip] = lax.dot_general(k_tile(j), q_strip(b, st), (((1,), (1,)), ((), ())), preferred_element_type=F32)
-
-    def update(src, j, st, rows, mask_off):
+    def scores(dst, mx, b, j, st, rows=tk, mask_off=None):
         sl = slice(st * strip, (st + 1) * strip)
-        s = src[0:rows, sl]
+        s = lax.dot_general(k_tile(j)[0:rows], q_strip(b, st), (((1,), (1,)), ((), ())), preferred_element_type=F32)
         if mask_off is not None:
             r = lax.broadcasted_iota(jnp.int32, (rows, strip), 0)
             q = lax.broadcasted_iota(jnp.int32, (rows, strip), 1)
             s = jnp.where(r <= q + mask_off, s, NEG_BIG)
+        dst[0:rows, sl] = s
+        mx[:, sl] = jnp.max(s, axis=0, keepdims=True)
+
+    def update(src, mx, j, st, rows=tk):
+        sl = slice(st * strip, (st + 1) * strip)
         m_old = m_ref[:, sl]
-        m_new = jnp.maximum(m_old, jnp.max(s, axis=0, keepdims=True))
+        m_new = jnp.maximum(m_old, mx[:, sl])
         alpha = jnp.exp2((m_old - m_new) * c_exp)
-        p = jnp.exp2((s - m_new) * c_exp)
+        p = jnp.exp2((src[0:rows, sl] - m_new) * c_exp)
         l_ref[:, sl] = l_ref[:, sl] * alpha + jnp.sum(p, axis=0, keepdims=True)
         m_ref[:, sl] = m_new
         acc_ref[:, sl] = acc_ref[:, sl] * alpha + jnp.dot(vt_tile(j, rows), p.astype(BF16), preferred_element_type=F32)
@@ -255,28 +257,55 @@
         m_ref[...] = jnp.full(m_ref.shape, NEG_BIG, F32)
         l_ref[...] = jnp.zeros(l_ref.shape, F32)
         acc_ref[...] = jnp.zeros(acc_ref.shape, F32)
+        half = n_strips // 2
+
+        def diag_scores(dst, mx, which, st):
+            d = st - which * half
+            if 0 <= d < half:
+                scores(dst, mx, b, 2 * b + which, st, (d + 1) * strip, d * strip)
+            elif d >= half:
+                scores(dst, mx, b, 2 * b + which, st)
+
+        def diag_update(src, mx, which, st):
+            d = st - which * half
+            if d >= 0:
+                update(src, mx, 2 * b + which, st, min(d + 1, half) * strip)
+
+        @pl.when(b > 0)
+        def _():
+            for st in range(n_strips):
+                scores(s0, x0, b, 0, st)
+
+        def pair(jj, _):
+            for st in range(n_strips):
+                scores(s1, x1, b, 2 * jj + 1, st)
+                update(s0, x0, 2 * jj, st)
+            for st in range(n_strips):
+                scores(s0, x0, b, 2 * jj + 2, st)
+                update(s1, x1, 2 * jj + 1, st)
+            return 0
+
+        lax.fori_loop(0, b - 1, pair, 0)
+
+        @pl.when(b > 0)
+        def _():
+            for st in range(n_strips):
+                scores(s1, x1, b, 2 * b - 1, st)
+                update(s0, x0, 2 * b - 2, st)
+            for st in range(n_strips):
+                diag_scores(s0, x0, 0, st)
+                update(s1, x1, 2 * b - 1, st)
+
+        @pl.when(b == 0)
+        def _():
+            for st in range(n_strips):
+                diag_scores(s0, x0, 0, st)
+
         for st in range(n_strips):
-            scores(s0, b, 0, st)
-
-        def pair(jj, _):
-            for st in range(n_strips):
-                scores(s1, b, 2 * jj + 1, st)
-                update(s0, 2 * jj, st, tk, None)
-            for st in range(n_strips):
-                scores(s0, b, 2 * jj + 2, st)
-                update(s1, 2 * jj + 1, st, tk, None)
-            return 0
-
-        lax.fori_loop(0, b, pair, 0)
-        half = n_strips // 2
+            diag_scores(s1, x1, 1, st)
+            diag_update(s0, x0, 0, st)
         for st in range(n_strips):
-            if st >= half:
-                scores(s1, b, 2 * b + 1, st)
-                update(s0, 2 * b, st, tk, None)
-            else:
-                update(s0, 2 * b, st, (st + 1) * strip, st * strip)
-        for st in range(half, n_strips):
-            update(s1, 2 * b + 1, st, (st + 1 - half) * strip, (st - half) * strip)
+            diag_update(s1, x1, 1, st)
 
         inv = 1.0 / l_ref[...]
         for u in range(qc):
@@ -301,8 +330,6 @@
     lax.fori_loop(0, n_q, q_block, 0)
     n_mine = 2 * (n_dev - 1)
     wait_bytes(o_stage.at[pl.ds(0, n_mine)], o_send)
-    for cp in w_copies:
-        pass
     wait_bytes(wbuf, w_sem)
     wait_bytes(o_stage.at[pl.ds(0, n_mine)], o_sem)
 
@@ -347,7 +374,7 @@
             scratch_shapes=[
                 pltpu.VMEM((PIECES, chunk, model_dim), BF16),
                 pltpu.VMEM((4, 512, n_inner, head_dim), BF16),
-                pltpu.VMEM((512, n_inner, head_dim), F32),
+                pltpu.VMEM((512 * n_inner, head_dim), F32),
                 pltpu.VMEM((n_inner // 2, model_dim, 6 * head_dim), BF16),
                 pltpu.VMEM((PIECES, n_inner, 3, chunk, head_dim), BF16),
                 pltpu.VMEM((PIECES, 2, 3, chunk, head_dim), BF16),
@@ -371,6 +398,8 @@
                 pltpu.VMEM((tk, tq), F32),
                 pltpu.VMEM((1, tq), F32),
                 pltpu.VMEM((1, tq), F32),
+                pltpu.VMEM((1, tq), F32),
+                pltpu.VMEM((1, tq), F32),
                 pltpu.VMEM((head_dim, tq), F32),
                 pltpu.VMEM((n_chunks, chunk, head_dim), BF16),
                 pltpu.VMEM((rows, n_heads * head_dim), BF16),

time: 223 us -> 173 us (0.78)
  Pallas kernels: 216 us -> 167 us
    pallas_call x1, Pallas kernels: 148 us -> 104 us  [device_step(): pl.pallas_call(functools.partial(qkv_kernel, n_outer, n_inner), out_shape...]
    pallas_call x1, Pallas kernels: 68.4 us -> 62.5 us  [device_step(): pl.pallas_call(functools.partial(attn_kernel, n_outer, n_inner, head_dim...]
where the time goes in v2:
time: 173 us
  Pallas kernels  167 us (97%)
  other arithmetic  3.32 us (2%)
  local copies, waits for them, and re-layouts  3.13 us (2%)
    pallas_call x1, Pallas kernels, device_step(): pl.pallas_call(functools.partial(qkv_kernel, n_outer, n_inner), out_shape...  104 us
    pallas_call x1, Pallas kernels, device_step(): pl.pallas_call(functools.partial(attn_kernel, n_outer, n_inner, head_dim...  62.5 us

profile of v2, /device:TPU:97, one launch (start us, length us, event | category | flops | bytes accessed | tf_op | source)
XLA Modules:
  0.0 173.2 jit_solution(11045263682771131529)
XLA Ops:
  0.0 0.1 add_convert_fusion
  0.1 1.9 %fusion = (f32[8,128,64]{2,1,0:T(8,128)S(1)}, f32[8,128,64]{2,1,0:T(8,128)S(1)}, f32[8,128,64]{2,1,0:T(8,128)S(1)}) fusion(f32[64]{0:T(128)S(1)} %multiply_power_fusion, f32[8,128]{1,0:T(8,128)S(1)} %add_convert_fusion), kind=kLoop, calls=%fused_computation.4 | loop fusion | flops 131072 | bytes 790784 | tf_op jit(solution)/shard_map/neg | solution.py:364
  2.0 1.3 pad_maximum_fusion
  3.3 104.2 %qkv_exchange.1.qkv_hbm = bf16[64,3,128,128]{3,2,1,0:T(8,128)(2,1)} custom-call(bf16[256,4096]{1,0:T(8,128)(2,1)} %hid_in.1, bf16[4096,32,128]{2,1,0:T(8,128)(2,1)} %wq.1, bf16[4096,32,128]{2,1,0:T(8,128)(2,1)} %wk.1, bf16[4096,32,128]{2,1,0:T(8,128)(2,1)} %wv.1, f32[8,128,128]{2,1,0:T(8,128)} %get-tuple-element.8.cos_ref, ...), custom_call_target="tpu_custom_call" | custom-call | tf_op jit(solution)/shard_map/qkv_exchange/pallas_call | solution.py:369
  107.5 62.5 %attn_out.1 = bf16[256,4096]{1,0:T(8,128)(2,1)} custom-call(bf16[64,3,128,128]{3,2,1,0:T(8,128)(2,1)} %qkv_exchange.1.qkv_hbm, bf16[4096,4096]{1,0:T(8,128)(2,1)} %bitcast.1), custom_call_target="tpu_custom_call" | custom-call | tf_op jit(solution)/shard_map/attn_out/pallas_call | solution.py:389
  170.1 3.1 %copy.7 = bf16[256,4096]{1,0:T(8,128)(2,1)} copy(bf16[256,4096]{1,0:T(8,128)(2,1)} %attn_out.1) | data formatting | bytes 4194304
  (2 shorter events, 0.0 us)

commit v3 on v0

v3 whole, which is shorter than its diff:
```python
import functools
import math

import jax
import jax.numpy as jnp
from jax import lax
from jax.experimental import pallas as pl
from jax.experimental.pallas import tpu as pltpu
from jax.sharding import PartitionSpec as P

ROPE_BASE = 500000.0
NEG_BIG = -1e30
MESH = pl.DeviceIdType.MESH
F32 = jnp.float32
BF16 = jnp.bfloat16

PIECES = 8
PIECE_HALF = (0, 1, 0, 0, 0, 1, 1, 1)
PIECE_DY = (0, 0, -1, 1, 2, -1, 1, 2)

PROJ, EARLY, FRONT, RECT, LAST = range(5)
STEPS = (
    (PROJ, 2), (PROJ, 3), (PROJ, 4), (EARLY, 0), (FRONT, 0), (FRONT, 1), (PROJ, 5), (PROJ, 6), (FRONT, 2), (PROJ, 7), (FRONT, 3),
    (RECT, -1), (RECT, 1), (RECT, 2), (LAST, 0), (LAST, 1), (LAST, 2), (LAST, 3),
)
STEP = {s: n for n, s in enumerate(STEPS)}
FORWARD = {STEP[PROJ, 3]: (2,), STEP[PROJ, 4]: (3,), STEP[EARLY, 0]: (4,), STEP[PROJ, 6]: (5,), STEP[FRONT, 2]: (6,), STEP[RECT, 1]: (7,)}
ARRIVE = {STEP[EARLY, 0]: (0, 1, 2, 3), STEP[FRONT, 0]: (4,), STEP[RECT, -1]: (5,), STEP[RECT, 1]: (6,), STEP[RECT, 2]: (7,)}


def lut(n, values):
    out = jnp.int32(values[-1])
    for k in range(len(values) - 2, -1, -1):
        if values[k] != values[k + 1] or k < len(values) - 2:
            out = jnp.where(n == k, jnp.int32(values[k]), out)
    return out


def remote(src, dst, send_sem, recv_sem, y, i):
    return pltpu.make_async_remote_copy(src_ref=src, dst_ref=dst, send_sem=send_sem, recv_sem=recv_sem, device_id={'cpo': y, 'cpi': i}, device_id_type=MESH)


def wait_bytes(ref, sem):
    pltpu.make_async_copy(ref, ref, sem).wait()


def layer_kernel(n_outer, n_inner, score_scale, hid_in, wq, wk, wv, wout, cos_ref, sin_ref, out_ref,
                 hid, raw, wide, big, stage, relay, qkv, s0, s1, x0, x1, m_ref, l_ref, acc_ref, o_recv,
                 h_send, h_recv, h_load, w_sem, s_send, r_send, r_recv, q_recv, wo_sem, o_send, o_sem):
    y = lax.axis_index('cpo')
    i = lax.axis_index('cpi')
    me = y * n_inner + i
    n_dev = n_outer * n_inner
    n_x = n_inner // 2
    x = i // 2
    c = lax.rem(i, 2)
    chunk, model_dim = hid.shape[1:]
    half_rows = chunk // 2
    head_dim = qkv.shape[2]
    n_chunks = qkv.shape[0]
    group = big.shape[2]
    depth = raw.shape[1]
    n_k = model_dim // depth
    n_raw = raw.shape[0]
    y_up = lax.rem(y + 1, n_outer)
    y_dn = lax.rem(y + n_outer - 1, n_outer)
    x_up = lax.rem(x + 1, n_x)
    x_dn = lax.rem(x + n_x - 1, n_x)
    x_far = lax.rem(x + 2, n_x)
    weights = (wq, wk, wv)
    tk, tq = s0.shape
    kc = tk // chunk
    qc = tq // chunk
    n_q = n_chunks // qc
    strip = 256
    n_strips = tq // strip
    half = n_strips // 2
    c_exp = score_scale * math.log2(math.e)

    def w_copy(t, k, slot):
        src = weights[t].at[pl.ds(k * depth, depth), pl.ds(pl.multiple_of(y * n_inner, n_inner), n_inner)]
        return pltpu.make_async_copy(src, raw.at[slot], w_sem.at[slot])

    for slot in range(n_raw):
        w_copy(0, slot, slot).start()
    own = [pltpu.make_async_copy(hid_in.at[pl.ds(f * chunk, chunk)], hid.at[f], h_load.at[f]) for f in range(2)]
    for cp in own:
        cp.start()

    barrier = pltpu.get_barrier_semaphore()

    def sig(d, _):
        peer = lax.rem(me + d, n_dev)
        pl.semaphore_signal(barrier, inc=1, device_id={'cpo': peer // n_inner, 'cpi': lax.rem(peer, n_inner)}, device_id_type=MESH)
        return 0

    lax.fori_loop(1, n_dev, sig, 0)
    pl.semaphore_wait(barrier, n_dev - 1)

    front = hid_in.at[pl.ds(0, chunk)]
    back = hid_in.at[pl.ds(chunk, chunk)]
    lo, hi = pl.ds(0, half_rows), pl.ds(half_rows, half_rows)
    send_front = [remote(front, hid.at[2], h_send.at[0], h_recv.at[2], y_up, i), remote(front, hid.at[3], h_send.at[1], h_recv.at[3], y_dn, i)]
    send_back = [remote(back, hid.at[5], h_send.at[2], h_recv.at[5], y_up, i), remote(back, hid.at[6], h_send.at[3], h_recv.at[6], y_dn, i)]
    fwd_front = [remote(hid.at[2, lo], hid.at[4, lo], h_send.at[4], h_recv.at[4], y_up, i), remote(hid.at[3, hi], hid.at[4, hi], h_send.at[5], h_recv.at[8], y_dn, i)]
    fwd_back = [remote(hid.at[5, lo], hid.at[7, lo], h_send.at[6], h_recv.at[7], y_up, i), remote(hid.at[6, hi], hid.at[7, hi], h_send.at[7], h_recv.at[9], y_dn, i)]
    for cp in send_front:
        cp.start()

    def chunk_index(p, src_i):
        rank = lax.rem(y + lut(p, PIECE_DY) + n_outer, n_outer) * n_inner + src_i
        return jnp.where(lut(p, PIECE_HALF) == 0, rank, n_chunks - 1 - rank)

    def forward_relay(p, t):
        for c2 in range(2):
            src_x, dst_x = (x_dn, x_up) if c2 == 0 else (x_up, x_dn)
            wait_bytes(relay.at[p, t, c2], r_recv.at[p, t, c2])
            remote(relay.at[p, t, c2], qkv.at[chunk_index(p, src_x * 2 + c), t], r_send, q_recv.at[p], y, dst_x * 2 + c2).start()

    def finish_heads(acc, p, t, j0):
        for u in range(acc.shape[1] // head_dim):
            a = acc[:, u * head_dim:(u + 1) * head_dim]
            if t < 2:
                stage[p, t, j0 + u] = (a * cos_ref[p] + pltpu.roll(a, head_dim // 2, 1) * sin_ref[p]).astype(BF16)
            else:
                stage[p, t, j0 + u] = a.T.astype(BF16)

    def send_piece(p, t):
        out_t = chunk_index(p, i)
        for c2 in range(2):
            via = x_up if c2 == 0 else x_dn
            remote(stage.at[p, t, x_far * 2 + c2], relay.at[p, t, c2], s_send, r_recv.at[p, t, c2], y, via * 2 + c).start()
        for xc in (x_up, x_dn):
            for c2 in range(2):
                remote(stage.at[p, t, xc * 2 + c2], qkv.at[out_t, t], s_send, q_recv.at[p], y, xc * 2 + c2).start()
        other = x * 2 + 1 - c
        remote(stage.at[p, t, other], qkv.at[out_t, t], s_send, q_recv.at[p], y, other).start()
        qkv[out_t, t] = stage[p, t, i]

    n_split = 2
    cols = group // n_split
    per_split = cols // head_dim

    for t in range(3):
        def relayout(k, _, t=t):
            slot = lax.rem(t * n_k + k, n_raw)
            w_copy(t, k, slot).wait()
            wide[...] = raw[slot].astype(F32).reshape(wide.shape)
            for j in range(n_inner):
                big[t, pl.ds(pl.multiple_of(k * depth, depth), depth), j * head_dim:(j + 1) * head_dim] = wide[pl.ds(j, depth, n_inner), :].astype(BF16)
            nxt = k + n_raw

            @pl.when(nxt < n_k)
            def _():
                w_copy(t, nxt, slot).start()

            if t < 2:
                @pl.when(nxt >= n_k)
                def _():
                    w_copy(t + 1, nxt - n_k, slot).start()
            return 0

        lax.fori_loop(0, n_k, relayout, 0)
        if t == 0:
            for cp in own:
                cp.wait()
        else:
            for p in range(2):
                forward_relay(p, t - 1)
        if t == 2:
            wait_bytes(hid.at[2], h_recv.at[2])
            wait_bytes(hid.at[3], h_recv.at[3])
            for cp in fwd_front + send_back:
                cp.start()

        def own_rows(n, _, t=t):
            w = big[t, :, pl.ds(pl.multiple_of(n * cols, cols), cols)]
            acc = jnp.dot(hid[0:2].reshape(2 * chunk, model_dim), w, preferred_element_type=F32)
            for p in range(2):
                finish_heads(acc[p * chunk:(p + 1) * chunk], p, t, n * per_split)
            return 0

        lax.fori_loop(0, n_split, own_rows, 0)
        for p in range(2):
            send_piece(p, t)

    def project(p):
        for t in range(3):
            for n in range(n_split):
                acc = jnp.dot(hid[p], big[t, :, n * cols:(n + 1) * cols], preferred_element_type=F32)
                finish_heads(acc, p, t, n * per_split)
            send_piece(p, t)

    def k_tile(j, rows):
        return qkv[pl.ds(j * kc, rows // chunk), 1].reshape(rows, head_dim)

    def vt_tile(j, rows):
        return jnp.concatenate([qkv[j * kc + u, 2] for u in range(rows // chunk)], axis=1)

    def q_strip(b, st):
        n = strip // chunk
        return qkv[pl.ds(b * qc + st * n, n), 0].reshape(strip, head_dim)

    def scores(dst, mx, b, j, st, rows=tk, mask_off=None):
        sl = slice(st * strip, (st + 1) * strip)
        s = lax.dot_general(k_tile(j, rows), q_strip(b, st), (((1,), (1,)), ((), ())), preferred_element_type=F32)
        if mask_off is not None:
            r = lax.broadcasted_iota(jnp.int32, (rows, strip), 0)
            q = lax.broadcasted_iota(jnp.int32, (rows, strip), 1)
            s = jnp.where(r <= q + mask_off, s, NEG_BIG)
        dst[0:rows, sl] = s
        mx[:, sl] = jnp.max(s, axis=0, keepdims=True)

    def update(src, mx, sidx, j, st, rows=tk):
        sl = slice(st * strip, (st + 1) * strip)
        m_old = m_ref[sidx, :, sl]
        m_new = jnp.maximum(m_old, mx[:, sl])
        alpha = jnp.exp2((m_old - m_new) * c_exp)
        p = jnp.exp2((src[0:rows, sl] - m_new) * c_exp)
        l_ref[sidx, :, sl] = l_ref[sidx, :, sl] * alpha + jnp.sum(p, axis=0, keepdims=True)
        m_ref[sidx, :, sl] = m_new
        acc_ref[sidx, :, sl] = acc_ref[sidx, :, sl] * alpha + jnp.dot(vt_tile(j, rows), p.astype(BF16), preferred_element_type=F32)

    def attend(b, sidx, n_kv, key_block, init, diag):
        @pl.when(init)
        def _():
            m_ref[sidx] = jnp.full(m_ref.shape[1:], NEG_BIG, F32)
            l_ref[sidx] = jnp.zeros(l_ref.shape[1:], F32)
            acc_ref[sidx] = jnp.zeros(acc_ref.shape[1:], F32)

        def diag_scores(dst, mx, which, st):
            d = st - which * half
            if 0 <= d < half:
                scores(dst, mx, b, 2 * b + which, st, (d + 1) * strip, d * strip)
            elif d >= half:
                scores(dst, mx, b, 2 * b + which, st)

        def diag_update(src, mx, which, st):
            d = st - which * half
            if d >= 0:
                update(src, mx, sidx, 2 * b + which, st, min(d + 1, half) * strip)

        @pl.when(n_kv > 0)
        def _():
            for st in range(n_strips):
                scores(s0, x0, b, 2 * key_block(0), st)

            def pair(jj, _):
                kb = key_block(jj)
                nxt = key_block(jj + 1)
                for st in range(n_strips):
                    scores(s1, x1, b, 2 * kb + 1, st)
                    update(s0, x0, sidx, 2 * kb, st)
                for st in range(n_strips):
                    scores(s0, x0, b, 2 * nxt, st)
                    update(s1, x1, sidx, 2 * kb + 1, st)
                return 0

            lax.fori_loop(0, n_kv - 1, pair, 0)
            kb = key_block(n_kv - 1)
            for st in range(n_strips):
                scores(s1, x1, b, 2 * kb + 1, st)
                update(s0, x0, sidx, 2 * kb, st)

            @pl.when(diag)
            def _():
                for st in range(n_strips):
                    diag_scores(s0, x0, 0, st)
                    update(s1, x1, sidx, 2 * kb + 1, st)

            @pl.when(jnp.logical_not(diag))
            def _():
                for st in range(n_strips):
                    update(s1, x1, sidx, 2 * kb + 1, st)

        @pl.when(n_kv == 0)
        def _():
            for st in range(n_strips):
                diag_scores(s0, x0, 0, st)

        @pl.when(diag)
        def _():
            for st in range(n_strips):
                diag_scores(s1, x1, 1, st)
                diag_update(s0, x0, 0, st)
            for st in range(n_strips):
                diag_update(s1, x1, 1, st)
            inv = 1.0 / l_ref[sidx]
            for u in range(qc):
                sl = slice(u * chunk, (u + 1) * chunk)
                qkv[b * qc + u, 0] = (acc_ref[sidx, :, sl] * inv[:, sl]).T.astype(BF16)

    o_cols = pl.ds(pl.multiple_of(me * head_dim, head_dim), head_dim)

    def send_out(b):
        def one(u, _):
            t = b * qc + u
            is_front = t < n_dev
            owner = jnp.where(is_front, t, 2 * n_dev - 1 - t)
            rows = pl.ds(pl.multiple_of(jnp.where(is_front, 0, chunk), chunk), chunk)

            @pl.when(owner == me)
            def _():
                o_recv[rows, o_cols] = qkv[t, 0]

            @pl.when(owner != me)
            def _():
                remote(qkv.at[t, 0], o_recv.at[rows, o_cols], o_send, o_sem.at[y], owner // n_inner, lax.rem(owner, n_inner)).start()
            return 0

        lax.fori_loop(0, qc, one, 0)

    def out_row(r):
        return lax.rem(y + 1 + r, n_outer)

    def wo_copies():
        res = []
        for r in range(n_outer - 1):
            for n in range(n_outer):
                src = wout.at[pl.ds(pl.multiple_of(out_row(r) * group, group), group), pl.ds(n * group, group)]
                res.append(pltpu.make_async_copy(src, big.at[r, pl.ds(n * group, group)], wo_sem.at[r]))
        for u in range(PIECES):
            src = wout.at[pl.ds(pl.multiple_of(y * group + u * chunk, chunk), chunk)]
            res.append(pltpu.make_async_copy(src, hid.at[u], wo_sem.at[n_outer - 1]))
        return res

    kinds = [k for k, _ in STEPS]
    args = [a for _, a in STEPS]

    def step(n, _):
        kind = lut(n, kinds)
        arg = lut(n, args)
        for m, ps in ARRIVE.items():
            @pl.when(n == m)
            def _(ps=ps):
                for p in ps:
                    wait_bytes(qkv.at[pl.ds(0, n_inner - 1)], q_recv.at[p])

        @pl.when(n == STEP[PROJ, 4])
        def _():
            wait_bytes(hid.at[4, lo], h_recv.at[4])
            wait_bytes(hid.at[4, hi], h_recv.at[8])

        @pl.when(n == STEP[PROJ, 5])
        def _():
            wait_bytes(hid.at[5], h_recv.at[5])
            wait_bytes(hid.at[6], h_recv.at[6])
            for cp in fwd_back:
                cp.start()

        @pl.when(n == STEP[PROJ, 7])
        def _():
            wait_bytes(hid.at[7, lo], h_recv.at[7])
            wait_bytes(hid.at[7, hi], h_recv.at[9])

        @pl.when(kind == PROJ)
        def _():
            project(arg)

        @pl.when(n == STEP[PROJ, 2])
        def _():
            for p in range(2):
                forward_relay(p, 2)

        @pl.when(n == STEP[PROJ, 7])
        def _():
            for cp in fwd_front + fwd_back:
                cp.wait_send()
            for cp in wo_copies():
                cp.start()

        @pl.when(kind != PROJ)
        def _():
            row = jnp.where(kind == EARLY, y, jnp.where(kind == RECT, lax.rem(y + arg + n_outer, n_outer), lax.rem(y + 1 + arg, n_outer)))
            b = jnp.where(kind == FRONT, row, n_q - 1 - row)
            own_last = jnp.logical_and(kind == LAST, row == y)
            n_kv = jnp.where(kind == EARLY, 3, jnp.where(kind == FRONT, row, jnp.where(kind == RECT, n_outer, n_outer - 1 - row + jnp.where(own_last, 1, 0))))

            def key_block(jj):
                early = lax.rem(y + jnp.where(jj == 0, 0, jnp.where(jj == 1, n_outer - 1, 1)), n_outer)
                last = jnp.where(own_last, jnp.where(jj == 0, lax.rem(y + 2, n_outer), n_outer - 1 + jj), n_outer + jj)
                return jnp.where(kind == EARLY, early, jnp.where(kind == LAST, last, jj))

            sidx = jnp.where(kind == FRONT, n_outer, row)
            attend(b, sidx, n_kv, key_block, kind != LAST, jnp.logical_or(kind == FRONT, kind == LAST))

            @pl.when(kind == LAST)
            def _():
                send_out(b)

        for m, ps in FORWARD.items():
            @pl.when(n == m)
            def _(ps=ps):
                for p in ps:
                    for t in range(3):
                        forward_relay(p, t)

        @pl.when(n == STEP[RECT, 1])
        def _():
            lax.fori_loop(0, n_outer, lambda k, _: (send_out(lax.rem(y + 1 + k, n_outer)), 0)[1], 0)
        return 0

    lax.fori_loop(0, len(STEPS), step, 0)

    def o_part(r):
        return o_recv[:, pl.ds(pl.multiple_of(out_row(r) * group, group), group)]

    rows = o_recv.shape[0]
    for r in range(n_outer - 1):
        wait_bytes(qkv.at[pl.ds(0, 2 * n_inner), 0], o_sem.at[out_row(r)])
        wait_bytes(big.at[r], wo_sem.at[r])
    per_buf = tk // rows

    def out_cols(n):
        return pl.ds(pl.multiple_of(n * group, group), group)

    for k, buf in enumerate((s0, s1)):
        def others(m, _, k=k, buf=buf):
            n = k * per_buf + m
            acc = None
            for r in range(n_outer - 1):
                d = jnp.dot(o_part(r), big[r, out_cols(n)], preferred_element_type=F32)
                acc = d if acc is None else acc + d
            buf[pl.ds(pl.multiple_of(m * rows, rows), rows)] = acc
            return 0

        lax.fori_loop(0, per_buf, others, 0)
    wait_bytes(qkv.at[pl.ds(0, 2 * (n_inner - 1)), 0], o_sem.at[y])
    wait_bytes(hid, wo_sem.at[n_outer - 1])
    for k, buf in enumerate((s0, s1)):
        def own_part(m, _, k=k, buf=buf):
            n = k * per_buf + m
            w = hid[:, :, out_cols(n)].reshape(group, group)
            acc = buf[pl.ds(pl.multiple_of(m * rows, rows), rows)] + jnp.dot(o_part(n_outer - 1), w, preferred_element_type=F32)
            out_ref[:, out_cols(n)] = acc.astype(BF16)
            return 0

        lax.fori_loop(0, per_buf, own_part, 0)

    for cp in send_front + send_back:
        cp.wait_send()
    wait_bytes(stage.at[:, :, pl.ds(0, n_inner - 1)], s_send)
    wait_bytes(relay, r_send)
    wait_bytes(qkv.at[pl.ds(0, 2 * (n_dev - 1)), 0], o_send)


def solution(mesh):
    n_outer = mesh.shape['cpo']
    n_inner = mesh.shape['cpi']
    n_dev = n_outer * n_inner

    def device_step(hidden, w_query, w_key, w_value, w_out):
        rows, model_dim = hidden.shape
        chunk = rows // 2
        n_heads, head_dim = w_query.shape[1:]
        n_chunks = 2 * n_dev
        y = lax.axis_index('cpo')
        i = lax.axis_index('cpi')
        rank = (y + jnp.array(PIECE_DY, jnp.int32)) % n_outer * n_inner + i
        t = jnp.where(jnp.array(PIECE_HALF, jnp.int32) == 0, rank, n_chunks - 1 - rank)
        pos = t[:, None] * chunk + jnp.arange(chunk, dtype=jnp.int32)
        half_dim = head_dim // 2
        inv_freq = ROPE_BASE ** (-(2.0 / head_dim) * jnp.arange(half_dim, dtype=F32))
        angles = pos.astype(F32)[..., None] * inv_freq
        cos_t, sin_t = jnp.cos(angles), jnp.sin(angles)
        cos_t = jnp.concatenate([cos_t, cos_t], axis=-1)
        sin_t = jnp.concatenate([-sin_t, sin_t], axis=-1)

        any_spec = pl.BlockSpec(memory_space=pl.ANY)
        vmem_spec = pl.BlockSpec(memory_space=pltpu.VMEM)
        dma = pltpu.SemaphoreType.DMA
        depth = 256
        tk, tq = 512, n_inner * chunk
        group = n_inner * head_dim
        return pl.pallas_call(
            functools.partial(layer_kernel, n_outer, n_inner, head_dim ** -0.5),
            out_shape=jax.ShapeDtypeStruct((rows, model_dim), BF16),
            in_specs=[any_spec] * 5 + [vmem_spec] * 2,
            out_specs=vmem_spec,
            scratch_shapes=[
                pltpu.VMEM((PIECES, chunk, model_dim), BF16),
                pltpu.VMEM((4, depth, n_inner, head_dim), BF16),
                pltpu.VMEM((depth * n_inner, head_dim), F32),
                pltpu.VMEM((3, model_dim, group), BF16),
                pltpu.VMEM((PIECES, 3, n_inner, chunk, head_dim), BF16),
                pltpu.VMEM((PIECES, 3, 2, chunk, head_dim), BF16),
                pltpu.VMEM((n_chunks, 3, chunk, head_dim), BF16),
                pltpu.VMEM((tk, tq), F32),
                pltpu.VMEM((tk, tq), F32),
                pltpu.VMEM((1, tq), F32),
                pltpu.VMEM((1, tq), F32),
                pltpu.VMEM((n_outer + 1, 1, tq), F32),
                pltpu.VMEM((n_outer + 1, 1, tq), F32),
                pltpu.VMEM((n_outer + 1, head_dim, tq), F32),
                pltpu.VMEM((rows, n_heads * head_dim), BF16),
                dma((8,)), dma((10,)), dma((2,)), dma((4,)), dma, dma, dma((PIECES, 3, 2)), dma((PIECES,)), dma((n_outer,)), dma, dma((n_outer,)),
            ],
            compiler_params=pltpu.CompilerParams(collective_id=0, has_side_effects=True, vmem_limit_bytes=63 * 2**20),
            name='layer',
        )(hidden, w_query, w_key, w_value, w_out.reshape(n_heads * head_dim, model_dim), cos_t, sin_t)

    row_spec = P(('dp', 'cpo', 'cpi'), None)
    weight_spec = P(None, None, None)
    return jax.shard_map(device_step, mesh=mesh, in_specs=(row_spec, weight_spec, weight_spec, weight_spec, weight_spec), out_specs=row_spec, check_vma=False)
```

time: 815 us -> 166 us (0.20); the launches traced: 805 us -> 165 us
  waiting for transfers between devices: 299 us -> 0 us
  matrix products: 208 us -> 0 us
  Pallas kernels: 0 us -> 158 us
  local copies, waits for them, and re-layouts: 158 us -> 3.13 us
  other arithmetic: 85.8 us -> 3.98 us
  blocking collectives: 31.8 us -> 0 us
  starting transfers between devices: 20.9 us -> 0 us
    ppermute x6 -> x0, waiting for transfers between devices: 267 us -> none  [outer_step(): kv_block = lax.ppermute(kv_block, 'cpo', shift_perm)]
    dot_general x14 -> x0, matrix products: 208 us -> none  [the longest x5 75.7 us: softmax_update(): jnp.einsum('qkgs,skd->qkgd', probs_blk.astype(jnp.bfloat16), values_blk,...]
    pallas_call x0 -> x1, Pallas kernels: none -> 158 us  [device_step(): pl.pallas_call(functools.partial(layer_kernel, n_outer, n_inner, head_dim...]
    unnamed x18 -> x1, local copies, waits for them, and re-layouts: 93 us -> 3.13 us
    reduce_sum x5 -> x0, other arithmetic: 61.3 us -> none  [softmax_update(): new_sum = run_sum * rescale + probs_blk.sum(axis=-1)]
    all_to_all x3 -> x0, waiting for transfers between devices: 31.8 us -> none  [to_heads(): tensor_in = lax.all_to_all(tensor_in, 'cpi', 3, 1, tiled=True)]
    all_to_all x1 -> x0, blocking collectives: 31.8 us -> none  [device_step(): lax.all_to_all(out_heads, 'cpi', 1, 3, tiled=True)]
    while x21 -> x0, local copies, waits for them, and re-layouts: 20.9 us -> none
  transfers between devices with their start and end apart: 9 -> 0, of which waited for: 8 -> 0; matrix products, arithmetic and copies ran while one was open for 7% -> 0% of each run, Pallas kernels for 0% -> 0%
where the time goes in v3:
time: 166 us; the launch traced here: 165 us
  Pallas kernels  158 us (95%)
  other arithmetic  3.98 us (2%)
  local copies, waits for them, and re-layouts  3.13 us (2%)
    pallas_call x1, Pallas kernels, device_step(): pl.pallas_call(functools.partial(layer_kernel, n_outer, n_inner, head_dim...  158 us

profile of v3, /device:TPU:97, one launch (start us, length us, event | category | flops | bytes accessed | tf_op | source)
XLA Modules:
  0.0 165.5 jit_solution(4918913782171663582)
XLA Ops:
  0.0 0.7 fusion.4
  0.7 0.1 add_convert_fusion
  0.8 1.9 %fusion = (f32[8,128,64]{2,1,0:T(8,128)S(1)}, f32[8,128,64]{2,1,0:T(8,128)S(1)}, f32[8,128,64]{2,1,0:T(8,128)S(1)}) fusion(f32[64]{0:T(128)S(1)} %multiply_power_fusion, f32[8,128]{1,0:T(8,128)S(1)} %add_convert_fusion), kind=kLoop, calls=%fused_computation.4 | loop fusion | flops 131072 | bytes 790784 | tf_op jit(solution)/shard_map/neg | solution.py:467
  2.7 1.3 pad_maximum_fusion
  4.0 158.3 %layer.1 = bf16[256,4096]{1,0:T(8,128)(2,1)} custom-call(bf16[256,4096]{1,0:T(8,128)(2,1)} %hid_in.1, bf16[4096,32,128]{2,1,0:T(8,128)(2,1)} %wq.1, bf16[4096,32,128]{2,1,0:T(8,128)(2,1)} %wk.1, bf16[4096,32,128]{2,1,0:T(8,128)(2,1)} %wv.1, bf16[4096,4096]{1,0:T(8,128)(2,1)} %bitcast.1, f32[8,128,128]{2,1,0:T(8,128)} %get-tuple-element.8.cos_ref, ...), custom_call_target="tpu_custom_call" | custom-call | tf_op jit(solution)/shard_map/layer/pallas_call | solution.py:475
  162.3 3.1 %copy.9 = bf16[256,4096]{1,0:T(8,128)(2,1)} copy(bf16[256,4096]{1,0:T(8,128)(2,1)} %layer.1) | data formatting | bytes 4194304
  (1 shorter events, 0.0 us)

commit v4 on v3

--- a/solution.py
+++ b/solution.py
@@ -20,12 +20,12 @@
 
 PROJ, EARLY, FRONT, RECT, LAST = range(5)
 STEPS = (
-    (PROJ, 2), (PROJ, 3), (PROJ, 4), (EARLY, 0), (FRONT, 0), (FRONT, 1), (PROJ, 5), (PROJ, 6), (FRONT, 2), (PROJ, 7), (FRONT, 3),
+    (PROJ, 2), (PROJ, 3), (EARLY, 0), (PROJ, 4), (EARLY, 1), (FRONT, 0), (FRONT, 1), (PROJ, 5), (PROJ, 6), (FRONT, 2), (PROJ, 7), (FRONT, 3),
     (RECT, -1), (RECT, 1), (RECT, 2), (LAST, 0), (LAST, 1), (LAST, 2), (LAST, 3),
 )
 STEP = {s: n for n, s in enumerate(STEPS)}
-FORWARD = {STEP[PROJ, 3]: (2,), STEP[PROJ, 4]: (3,), STEP[EARLY, 0]: (4,), STEP[PROJ, 6]: (5,), STEP[FRONT, 2]: (6,), STEP[RECT, 1]: (7,)}
-ARRIVE = {STEP[EARLY, 0]: (0, 1, 2, 3), STEP[FRONT, 0]: (4,), STEP[RECT, -1]: (5,), STEP[RECT, 1]: (6,), STEP[RECT, 2]: (7,)}
+FORWARD = {STEP[PROJ, 3]: (2,), STEP[PROJ, 4]: (3,), STEP[EARLY, 1]: (4,), STEP[PROJ, 6]: (5,), STEP[FRONT, 2]: (6,), STEP[RECT, -1]: (7,)}
+ARRIVE = {STEP[EARLY, 0]: (0, 1), STEP[EARLY, 1]: (2, 3), STEP[FRONT, 0]: (4,), STEP[RECT, -1]: (5,), STEP[RECT, 1]: (6,), STEP[RECT, 2]: (7,)}
 
 
 def lut(n, values):
@@ -95,7 +95,6 @@
         return 0
 
     lax.fori_loop(1, n_dev, sig, 0)
-    pl.semaphore_wait(barrier, n_dev - 1)
 
     front = hid_in.at[pl.ds(0, chunk)]
     back = hid_in.at[pl.ds(chunk, chunk)]
@@ -104,8 +103,6 @@
     send_back = [remote(back, hid.at[5], h_send.at[2], h_recv.at[5], y_up, i), remote(back, hid.at[6], h_send.at[3], h_recv.at[6], y_dn, i)]
     fwd_front = [remote(hid.at[2, lo], hid.at[4, lo], h_send.at[4], h_recv.at[4], y_up, i), remote(hid.at[3, hi], hid.at[4, hi], h_send.at[5], h_recv.at[8], y_dn, i)]
     fwd_back = [remote(hid.at[5, lo], hid.at[7, lo], h_send.at[6], h_recv.at[7], y_up, i), remote(hid.at[6, hi], hid.at[7, hi], h_send.at[7], h_recv.at[9], y_dn, i)]
-    for cp in send_front:
-        cp.start()
 
     def chunk_index(p, src_i):
         rank = lax.rem(y + lut(p, PIECE_DY) + n_outer, n_outer) * n_inner + src_i
@@ -162,17 +159,14 @@
 
         lax.fori_loop(0, n_k, relayout, 0)
         if t == 0:
+            pl.semaphore_wait(barrier, n_dev - 1)
+            for cp in send_front:
+                cp.start()
             for cp in own:
                 cp.wait()
         else:
             for p in range(2):
                 forward_relay(p, t - 1)
-        if t == 2:
-            wait_bytes(hid.at[2], h_recv.at[2])
-            wait_bytes(hid.at[3], h_recv.at[3])
-            for cp in fwd_front + send_back:
-                cp.start()
-
         def own_rows(n, _, t=t):
             w = big[t, :, pl.ds(pl.multiple_of(n * cols, cols), cols)]
             acc = jnp.dot(hid[0:2].reshape(2 * chunk, model_dim), w, preferred_element_type=F32)
@@ -183,6 +177,11 @@
         lax.fori_loop(0, n_split, own_rows, 0)
         for p in range(2):
             send_piece(p, t)
+
+    wait_bytes(hid.at[2], h_recv.at[2])
+    wait_bytes(hid.at[3], h_recv.at[3])
+    for cp in fwd_front + send_back:
+        cp.start()
 
     def project(p):
         for t in range(3):
@@ -221,7 +220,7 @@
         m_ref[sidx, :, sl] = m_new
         acc_ref[sidx, :, sl] = acc_ref[sidx, :, sl] * alpha + jnp.dot(vt_tile(j, rows), p.astype(BF16), preferred_element_type=F32)
 
-    def attend(b, sidx, n_kv, key_block, init, diag):
+    def attend(b, sidx, n_kv, key_block, init, diag, finish):
         @pl.when(init)
         def _():
             m_ref[sidx] = jnp.full(m_ref.shape[1:], NEG_BIG, F32)
@@ -285,6 +284,9 @@
                 diag_update(s0, x0, 0, st)
             for st in range(n_strips):
                 diag_update(s1, x1, 1, st)
+
+        @pl.when(finish)
+        def _():
             inv = 1.0 / l_ref[sidx]
             for u in range(qc):
                 sl = slice(u * chunk, (u + 1) * chunk)
@@ -374,17 +376,22 @@
             row = jnp.where(kind == EARLY, y, jnp.where(kind == RECT, lax.rem(y + arg + n_outer, n_outer), lax.rem(y + 1 + arg, n_outer)))
             b = jnp.where(kind == FRONT, row, n_q - 1 - row)
             own_last = jnp.logical_and(kind == LAST, row == y)
-            n_kv = jnp.where(kind == EARLY, 3, jnp.where(kind == FRONT, row, jnp.where(kind == RECT, n_outer, n_outer - 1 - row + jnp.where(own_last, 1, 0))))
+            n_early = jnp.where(arg == 0, 1, 2)
+            n_last = n_outer - 1 - row + jnp.where(own_last, 1, 0)
+            n_kv = jnp.where(kind == EARLY, n_early, jnp.where(kind == FRONT, row, jnp.where(kind == RECT, n_outer, n_last)))
 
             def key_block(jj):
-                early = lax.rem(y + jnp.where(jj == 0, 0, jnp.where(jj == 1, n_outer - 1, 1)), n_outer)
+                early = jnp.where(arg == 0, y, jnp.where(jj == 0, y_dn, y_up))
                 last = jnp.where(own_last, jnp.where(jj == 0, lax.rem(y + 2, n_outer), n_outer - 1 + jj), n_outer + jj)
                 return jnp.where(kind == EARLY, early, jnp.where(kind == LAST, last, jj))
 
             sidx = jnp.where(kind == FRONT, n_outer, row)
-            attend(b, sidx, n_kv, key_block, kind != LAST, jnp.logical_or(kind == FRONT, kind == LAST))
-
-            @pl.when(kind == LAST)
+            finish = jnp.logical_or(kind == FRONT, kind == LAST)
+            init = jnp.logical_and(kind != LAST, jnp.logical_not(jnp.logical_and(kind == EARLY, arg == 1)))
+            diag = jnp.logical_or(jnp.logical_and(finish, jnp.logical_not(own_last)), jnp.logical_and(kind == EARLY, arg == 0))
+            attend(b, sidx, n_kv, key_block, init, diag, finish)
+
+            @pl.when(finish)
             def _():
                 send_out(b)
 
@@ -395,9 +402,6 @@
                     for t in range(3):
                         forward_relay(p, t)
 
-        @pl.when(n == STEP[RECT, 1])
-        def _():
-            lax.fori_loop(0, n_outer, lambda k, _: (send_out(lax.rem(y + 1 + k, n_outer)), 0)[1], 0)
         return 0
 
     lax.fori_loop(0, len(STEPS), step, 0)
@@ -460,11 +464,11 @@
         t = jnp.where(jnp.array(PIECE_HALF, jnp.int32) == 0, rank, n_chunks - 1 - rank)
         pos = t[:, None] * chunk + jnp.arange(chunk, dtype=jnp.int32)
         half_dim = head_dim // 2
-        inv_freq = ROPE_BASE ** (-(2.0 / head_dim) * jnp.arange(half_dim, dtype=F32))
+        lane = jnp.arange(head_dim, dtype=jnp.int32)
+        inv_freq = ROPE_BASE ** (-(2.0 / head_dim) * (lane % half_dim).astype(F32))
         angles = pos.astype(F32)[..., None] * inv_freq
-        cos_t, sin_t = jnp.cos(angles), jnp.sin(angles)
-        cos_t = jnp.concatenate([cos_t, cos_t], axis=-1)
-        sin_t = jnp.concatenate([-sin_t, sin_t], axis=-1)
+        cos_t = jnp.cos(angles)
+        sin_t = jnp.sin(angles) * jnp.where(lane < half_dim, -1.0, 1.0)
 
         any_spec = pl.BlockSpec(memory_space=pl.ANY)
         vmem_spec = pl.BlockSpec(memory_space=pltpu.VMEM)

time: 166 us -> 163 us (0.982)
  the two profiles are of different devices: /device:TPU:97 before, /device:TPU:112 now
where the time goes in v4:
time: 163 us
  Pallas kernels  156 us (96%)
  other arithmetic  3.8 us (2%)
  local copies, waits for them, and re-layouts  3.13 us (2%)
    pallas_call x1, Pallas kernels, device_step(): pl.pallas_call(functools.partial(layer_kernel, n_outer, n_inner, head_dim...  156 us

profile of v4, /device:TPU:112, one launch (start us, length us, event | category | flops | bytes accessed | tf_op | source)
XLA Modules:
  0.0 162.8 jit_solution(7299147921712106514)
XLA Ops:
  0.0 0.7 fusion.4
  0.7 0.1 add_convert_fusion
  0.8 3.0 %fusion = (f32[8,128,128]{2,1,0:T(8,128)}, f32[8,128,128]{2,1,0:T(8,128)}) fusion(f32[128]{0:T(128)S(1)} %get-tuple-element.7, f32[128]{0:T(128)S(1)} %get-tuple-element.8, f32[8,128]{1,0:T(8,128)S(1)} %add_convert_fusion), kind=kLoop, calls=%fused_computation.2 | loop fusion | flops 262144 | bytes 1053696 | tf_op jit(solution)/shard_map/mul | solution.py:471
  3.8 155.9 %layer.1 = bf16[256,4096]{1,0:T(8,128)(2,1)} custom-call(bf16[256,4096]{1,0:T(8,128)(2,1)} %hid_in.1, bf16[4096,32,128]{2,1,0:T(8,128)(2,1)} %wq.1, bf16[4096,32,128]{2,1,0:T(8,128)(2,1)} %wk.1, bf16[4096,32,128]{2,1,0:T(8,128)(2,1)} %wv.1, bf16[4096,4096]{1,0:T(8,128)(2,1)} %bitcast.1, f32[8,128,128]{2,1,0:T(8,128)} %get-tuple-element.6.cos_ref, ...), custom_call_target="tpu_custom_call" | custom-call | tf_op jit(solution)/shard_map/layer/pallas_call | solution.py:479
  159.7 3.1 %copy.9 = bf16[256,4096]{1,0:T(8,128)(2,1)} copy(bf16[256,4096]{1,0:T(8,128)(2,1)} %layer.1) | data formatting | bytes 4194304
  (1 shorter events, 0.0 us)
